TPU v7x, 32 devices: a whole 2x2x4 slice. The times are simulated.
32 devices in a mesh: dp: 32 (over z, y, x, core).
Axes of the slice: x: 2, y: 2, z: 4, core: 2. Of those that a mesh axis runs over, the one named last changes fastest.
Arguments:
- x_rows: bfloat16 [131072, 576], P('dp')
- dy_rows: bfloat16 [131072, 576], P('dp')
- w_one: bfloat16 [576, 6144], replicated
- w_two: bfloat16 [6144, 576], replicated
- w_three: bfloat16 [576, 1536], replicated
- w_four: bfloat16 [1536, 576], replicated
- master_one: float32 [576, 6144], P('dp')
- master_two: float32 [6144, 576], P('dp')
- master_three: float32 [576, 1536], P('dp')
- master_four: float32 [1536, 576], P('dp')
- m_one: float32 [576, 6144], P('dp')
- m_two: float32 [6144, 576], P('dp')
- m_three: float32 [576, 1536], P('dp')
- m_four: float32 [1536, 576], P('dp')
- v_one: float32 [576, 6144], P('dp')
- v_two: float32 [6144, 576], P('dp')
- v_three: float32 [576, 1536], P('dp')
- v_four: float32 [1536, 576], P('dp')
- learn_rate: float32 [], replicated
- clip_max: float32 [], replicated
Outputs:
- output 1: bfloat16 [576, 6144], replicated
- output 2: bfloat16 [6144, 576], replicated
- output 3: bfloat16 [576, 1536], replicated
- output 4: bfloat16 [1536, 576], replicated
- output 5: float32 [576, 6144], P('dp')
- output 6: float32 [6144, 576], P('dp')
- output 7: float32 [576, 1536], P('dp')
- output 8: float32 [1536, 576], P('dp')
- output 9: float32 [576, 6144], P('dp')
- output 10: float32 [6144, 576], P('dp')
- output 11: float32 [576, 1536], P('dp')
- output 12: float32 [1536, 576], P('dp')
- output 13: float32 [576, 6144], P('dp')
- output 14: float32 [6144, 576], P('dp')
- output 15: float32 [576, 1536], P('dp')
- output 16: float32 [1536, 576], P('dp')
- output 17: float32 [], replicated
All inputs are finite; a program needn't handle non-finite values.
Results may differ from a plain program's by a relative error of at most 0.0126751.
Values are sent between devices in bfloat16 or wider.
A program may use at most 1 GiB of HBM per device.

v0:
```python
import jax
import jax.numpy as jnp
from jax import lax
from jax.sharding import PartitionSpec as P

ADAM_STEP = 10
BETA_ONE = 0.9
BETA_TWO = 0.95
ADAM_EPS = 1e-8
NORM_EPS = 1e-6
BIAS_ONE = 1.0 - BETA_ONE ** ADAM_STEP
BIAS_TWO = 1.0 - BETA_TWO ** ADAM_STEP
INV_SQRT2 = 0.7071067811865476
INV_SQRT2PI = 0.3989422804014327


def gelu_value(pre_act):
    pre_wide = pre_act.astype(jnp.float32)
    return 0.5 * pre_wide * (1.0 + lax.erf(pre_wide * INV_SQRT2))


def gelu_slope(pre_act):
    pre_wide = pre_act.astype(jnp.float32)
    return 0.5 * (1.0 + lax.erf(pre_wide * INV_SQRT2)) + pre_wide * INV_SQRT2PI * jnp.exp(-0.5 * pre_wide * pre_wide)


def local_grads(x_rows, dy_rows, w_one, w_two, w_three, w_four):
    z_one = jnp.dot(x_rows, w_one, preferred_element_type=jnp.float32).astype(jnp.bfloat16)
    a_one = gelu_value(z_one).astype(jnp.bfloat16)
    h_two = jnp.dot(a_one, w_two, preferred_element_type=jnp.float32).astype(jnp.bfloat16)
    z_three = jnp.dot(h_two, w_three, preferred_element_type=jnp.float32).astype(jnp.bfloat16)
    a_three = gelu_value(z_three).astype(jnp.bfloat16)
    g_four = jnp.einsum('rf,rd->fd', a_three, dy_rows, preferred_element_type=jnp.float32)
    da_three = jnp.einsum('rd,fd->rf', dy_rows, w_four, preferred_element_type=jnp.float32).astype(jnp.bfloat16)
    dz_three = (da_three.astype(jnp.float32) * gelu_slope(z_three)).astype(jnp.bfloat16)
    g_three = jnp.einsum('rd,rf->df', h_two, dz_three, preferred_element_type=jnp.float32)
    dh_two = jnp.einsum('rf,df->rd', dz_three, w_three, preferred_element_type=jnp.float32).astype(jnp.bfloat16)
    g_two = jnp.einsum('rw,rd->wd', a_one, dh_two, preferred_element_type=jnp.float32)
    da_one = jnp.einsum('rd,wd->rw', dh_two, w_two, preferred_element_type=jnp.float32).astype(jnp.bfloat16)
    dz_one = (da_one.astype(jnp.float32) * gelu_slope(z_one)).astype(jnp.bfloat16)
    g_one = jnp.einsum('rd,rw->dw', x_rows, dz_one, preferred_element_type=jnp.float32)
    return g_one, g_two, g_three, g_four


def adam_rows(grad_mat, master_mat, mom_mat, var_mat, clip_scale, learn_rate):
    scaled = clip_scale * grad_mat
    mom_new = BETA_ONE * mom_mat + (1.0 - BETA_ONE) * scaled
    var_new = BETA_TWO * var_mat + (1.0 - BETA_TWO) * scaled * scaled
    master_new = master_mat - learn_rate * (mom_new / BIAS_ONE) / (jnp.sqrt(var_new / BIAS_TWO) + ADAM_EPS)
    return master_new, mom_new, var_new


def solution(mesh):
    dp_size = mesh.shape['dp']
    row_spec = P('dp', None)
    rep_spec = P()

    def per_device(x_rows, dy_rows, w_one, w_two, w_three, w_four, master_one, master_two, master_three, master_four, m_one, m_two, m_three, m_four, v_one, v_two, v_three, v_four, learn_rate, clip_max):
        grads = local_grads(x_rows, dy_rows, w_one, w_two, w_three, w_four)
        shards = [lax.psum_scatter(grad_mat, 'dp', scatter_dimension=0, tiled=True) / dp_size for grad_mat in grads]
        local_sq = sum(jnp.sum(shard_mat * shard_mat) for shard_mat in shards)
        grad_norm = jnp.sqrt(lax.psum(local_sq, 'dp'))
        clip_scale = jnp.minimum(1.0, clip_max / (grad_norm + NORM_EPS))
        results = [adam_rows(shard_mat, master_mat, mom_mat, var_mat, clip_scale, learn_rate) for shard_mat, master_mat, mom_mat, var_mat in zip(shards, (master_one, master_two, master_three, master_four), (m_one, m_two, m_three, m_four), (v_one, v_two, v_three, v_four))]
        new_weights = tuple(lax.all_gather(result[0].astype(jnp.bfloat16), 'dp', axis=0, tiled=True) for result in results)
        return new_weights + tuple(result[0] for result in results) + tuple(result[1] for result in results) + tuple(result[2] for result in results) + (grad_norm,)

    in_specs = (row_spec, row_spec) + (rep_spec,) * 4 + (row_spec,) * 12 + (rep_spec, rep_spec)
    out_specs = (rep_spec,) * 4 + (row_spec,) * 12 + (rep_spec,)
    return jax.shard_map(per_device, mesh=mesh, in_specs=in_specs, out_specs=out_specs, check_vma=False)
```

profile of v0, /device:TPU:9, one launch (start us, length us, event | category | flops | bytes accessed | tf_op | source)
XLA Modules:
  0.0 1161.8 jit_solution(9939397439191470602)
XLA Ops:
  7.3 62.0 %fusion.5 = (f32[4096,6144]{1,0:T(8,128)}, bf16[4096,6144]{1,0:T(8,128)(2,1)}) fusion(bf16[4096,576]{0,1:T(8,128)(2,1)} %param.20, bf16[576,6144]{1,0:T(8,128)(2,1)} %param.22), kind=kOutput, calls=%fused_computation.8 | convolution fusion | flops 29091692544 | bytes 162791424 | tf_op jit(solution)/shard_map/dot_general | solution.py:28
  69.3 52.4 %convolution_convert_fusion.4 = bf16[4096,576]{0,1:T(8,128)(2,1)} fusion(bf16[6144,576]{0,1:T(8,128)(2,1)} %param.23, f32[4096,6144]{1,0:T(8,128)} %get-tuple-element.88, bf16[4096,6144]{1,0:T(8,128)(2,1)} %get-tuple-element.89), kind=kOutput, calls=%fused_computation.36 | convolution fusion | flops 29094051840 | bytes 162791424 | tf_op jit(solution)/shard_map/dot_general | solution.py:30
  121.7 13.6 %convolution_convert_fusion.1 = bf16[4096,1536]{1,0:T(8,128)(2,1)S(1)} fusion(bf16[4096,576]{0,1:T(8,128)(2,1)} %convolution_convert_fusion.4, bf16[576,1536]{1,0:T(8,128)(2,1)S(1)} %copy-done), kind=kOutput, calls=%fused_computation.30 | convolution fusion | flops 7254048768 | bytes 19070976 | tf_op jit(solution)/shard_map/dot_general | solution.py:31
  139.8 13.8 %fusion.22 = f32[1536,576]{1,0:T(8,128)} fusion(bf16[4096,576]{0,1:T(8,128)(2,1)S(1)} %copy-done.16, bf16[4096,1536]{1,0:T(8,128)(2,1)S(1)} %convolution_convert_fusion.1), kind=kOutput, calls=%fused_computation.32 | convolution fusion | flops 7285506048 | bytes 20840448 | tf_op jit(solution)/shard_map/rf,rd->fd/dot_general | solution.py:33
  153.7 21.6 %fusion.18 = bf16[4096,1536]{1,0:T(8,128)(2,1)S(1)} fusion(bf16[4096,1536]{1,0:T(8,128)(2,1)} %copy-done.19, bf16[4096,576]{0,1:T(8,128)(2,1)} %param.21, bf16[1536,576]{0,1:T(8,128)(2,1)S(1)} %copy-done.17), kind=kOutput, calls=%fused_computation.26 | convolution fusion | flops 7329546240 | bytes 31653888 | tf_op jit(solution)/shard_map/rd,fd->rf/dot_general | solution.py:34
  179.8 13.8 %convolution_convert_fusion.3 = bf16[4096,576]{0,1:T(8,128)(2,1)} fusion(bf16[4096,1536]{1,0:T(8,128)(2,1)S(1)} %fusion.18, bf16[576,1536]{1,0:T(8,128)(2,1)S(1)} %copy-done), kind=kOutput, calls=%fused_computation.35 | convolution fusion | flops 7250116608 | bytes 19070976 | tf_op jit(solution)/shard_map/rf,df->rd/dot_general | solution.py:37
  193.5 58.5 %fusion.36 = f32[6144,576]{1,0:T(8,128)} fusion(bf16[4096,576]{0,1:T(8,128)(2,1)} %convolution_convert_fusion.3, f32[4096,6144]{1,0:T(8,128)} %get-tuple-element.88, bf16[4096,6144]{1,0:T(8,128)(2,1)} %get-tuple-element.89), kind=kOutput, calls=%fused_computation.63 | convolution fusion | flops 29091692544 | bytes 169869312 | tf_op jit(solution)/shard_map/rw,rd->wd/dot_general | solution.py:38
  252.1 48.0 %fusion.47 = bf16[4096,6144]{1,0:T(8,128)(2,1)} fusion(bf16[4096,576]{0,1:T(8,128)(2,1)} %convolution_convert_fusion.3, bf16[6144,576]{0,1:T(8,128)(2,1)} %param.23), kind=kOutput, calls=%fused_computation.66 | convolution fusion | flops 28991029248 | bytes 62128128 | tf_op jit(solution)/shard_map/rd,wd->rw/dot_general | solution.py:39
  300.1 13.4 %fusion.48 = f32[576,1536]{1,0:T(8,128)} fusion(bf16[4096,576]{0,1:T(8,128)(2,1)} %convolution_convert_fusion.4, bf16[4096,1536]{1,0:T(8,128)(2,1)} %copy-done.18), kind=kOutput, calls=%fused_computation.67 | convolution fusion | flops 7247757312 | bytes 20840448 | tf_op jit(solution)/shard_map/rd,rf->df/dot_general | solution.py:36
  313.5 70.9 %fusion.25 = f32[576,6144]{1,0:T(8,128)} fusion(bf16[4096,576]{0,1:T(8,128)(2,1)} %param.20, bf16[4096,6144]{1,0:T(8,128)(2,1)} %get-tuple-element.89, f32[4096,6144]{1,0:T(8,128)} %get-tuple-element.88, bf16[4096,6144]{1,0:T(8,128)(2,1)} %fusion.47), kind=kOutput, calls=%fused_computation.34 | convolution fusion | flops 29242687488 | bytes 220200960 | tf_op jit(solution)/shard_map/rd,rw->dw/dot_general | solution.py:41
  384.4 260.4 %fusion.40 = (f32[24,6144]{1,0:T(8,128)S(1)}, f32[24,1536]{1,0:T(8,128)S(1)}) fusion(f32[576,6144]{1,0:T(8,128)} %fusion.25, f32[576,1536]{1,0:T(8,128)} %fusion.48), kind=kCustom, calls=%all-reduce-scatter.2 | all-reduce-scatter fusion | flops 5898241 | bytes 18432000
  650.8 6.3 collective-permute-start.5
  662.9 24.3 %collective-permute-start.12 = (f32[24,1536]{1,0:T(8,128)S(1)}, f32[24,1536]{1,0:T(8,128)S(1)}, u32[]{:S(2)}, u32[]{:S(2)}) collective-permute-start(f32[24,1536]{1,0:T(8,128)S(1)} %get-tuple-element.71), channel_id=1, source_target_pairs={{0,5},{1,6},{2,7},{3,8},{4,9},{5,10},{6,11},{7,12},{8,13},{9,14},{... | collective-permute-start | bytes 442376
  696.7 11.4 collective-permute-done.11
  743.2 20.7 %collective-permute-done.3 = f32[24,6144]{1,0:T(8,128)} collective-permute-done((f32[24,6144]{1,0:T(8,128)S(1)}, f32[24,6144]{1,0:T(8,128)}, u32[]{:S(2)}, u32[]{:S(2)}) %collective-permute-start.3) | collective-permute-done | bytes 589856
  763.9 7.4 collective-permute-done.2
  774.2 36.8 %concatenate = f32[210,6144]{1,0:T(8,128)} concatenate(f32[18,6144]{1,0:T(8,128)} %copy-done.4, f32[24,6144]{1,0:T(8,128)} %copy-done.2, f32[24,6144]{1,0:T(8,128)} %copy-done.3, f32[24,6144]{1,0:T(8,128)} %collective-permute-done.4, f32[24,6144]{1,0:T(8,128)} %collective-permute-done.3, f32[24,6144]{1,0:T(8,128)S(1)} %collective-permute-done.2, ...), dimensions={0} | concatenate | bytes 10321920
  818.7 45.6 %psum.7 = f32[]{:T(128)} all-reduce(f32[]{:T(128)S(6)} %add.90), channel_id=1, replica_groups=mesh['dp'=32] {'dp'}, use_global_device_ids=true, to_apply=%region_8.0 | all-reduce | flops 1 | bytes 8 | tf_op jit(solution)/shard_map/psum | solution.py:62
  874.0 49.5 %all-gather.13.cloned.1.call-done = bf16[32,18,1536]{2,1,0:T(8,128)(2,1)} async-done(((bf16[1,18,1536]{2,1,0:T(8,128)(2,1)}), bf16[32,18,1536]{2,1,0:T(8,128)(2,1)}) %all-gather.13.cloned.1.call-update) | async-done | bytes 1769488 | tf_op jit(solution)/shard_map/all_gather | solution.py:65
  927.4 53.7 %all-gather.9.cloned.1.call-done = bf16[1536,576]{1,0:T(8,128)(2,1)} async-done(((bf16[48,576]{1,0:T(8,128)(2,1)}), bf16[1536,576]{1,0:T(8,128)(2,1)}) %all-gather.9.cloned.1.call-update) | async-done | bytes 1769488 | tf_op jit(solution)/shard_map/all_gather | solution.py:65
  985.0 80.7 %all-gather.11.cloned.1.call-done = bf16[32,18,6144]{2,1,0:T(8,128)(2,1)} async-done(((bf16[1,18,6144]{2,1,0:T(8,128)(2,1)}), bf16[32,18,6144]{2,1,0:T(8,128)(2,1)}) %all-gather.11.cloned.1.call-update) | async-done | bytes 7077904 | tf_op jit(solution)/shard_map/all_gather | solution.py:65
  1065.7 9.6 reshape.35
  1075.3 67.9 %all-gather.7.cloned.1.call-done = bf16[6144,576]{1,0:T(8,128)(2,1)} async-done(((bf16[192,576]{1,0:T(8,128)(2,1)}), bf16[6144,576]{1,0:T(8,128)(2,1)}) %all-gather.7.cloned.1.call-update) | async-done | bytes 7077904 | tf_op jit(solution)/shard_map/all_gather | solution.py:65
  1143.2 10.5 copy.41
  (94 shorter events, 88.6 us)
Async XLA Ops:
  7.2 805.6 %reduce-scatter.9.cloned.1.call-start = ((), (), s32[]{:S(2)}) async-start(), calls=%async_computation.3 | async-start | bytes 4055040 | tf_op jit(solution)/shard_map/reduce_scatter | solution.py:60
  153.6 660.7 %reduce-scatter.7.cloned.1.call-start = ((), (), s32[]{:S(2)}) async-start(), calls=%async_computation.2 | async-start | bytes 16220160 | tf_op jit(solution)/shard_map/reduce_scatter | solution.py:60
  252.0 671.5 %all-gather.13.cloned.1.call-start = ((), (), s32[]{:S(2)}) async-start(), calls=%async_computation.7 | async-start | bytes 2433024 | tf_op jit(solution)/shard_map/all_gather | solution.py:65
  644.9 220.2 %copy-start.5 = (f32[18,1536]{1,0:T(8,128)S(1)}, f32[18,1536]{1,0:T(8,128)}, u32[]{:S(2)}) copy-start(f32[18,1536]{1,0:T(8,128)} %param.28) | copy-start | bytes 331780
  644.9 220.2 %copy-start.6 = (f32[18,1536]{1,0:T(8,128)S(1)}, f32[18,1536]{1,0:T(8,128)}, u32[]{:S(2)}) copy-start(f32[18,1536]{1,0:T(8,128)} %param.32) | copy-start | bytes 331780
  644.9 42.4 %collective-permute-start.14 = (f32[24,1536]{1,0:T(8,128)S(1)}, f32[24,1536]{1,0:T(8,128)S(1)}, u32[]{:S(2)}, u32[]{:S(2)}) collective-permute-start(f32[24,1536]{1,0:T(8,128)S(1)} %get-tuple-element.71), channel_id=1, source_target_pairs={{0,7},{1,8},{2,9},{3,10},{4,11},{5,12},{6,13},{7,14},{8,15},{9,16}... | collective-permute-start | bytes 442376
  647.0 83.2 %collective-permute-start.6 = (f32[24,6144]{1,0:T(8,128)S(1)}, f32[24,6144]{1,0:T(8,128)S(1)}, u32[]{:S(2)}, u32[]{:S(2)}) collective-permute-start(f32[24,6144]{1,0:T(8,128)S(1)} %get-tuple-element.70), channel_id=1, source_target_pairs={{0,7},{1,8},{2,9},{3,10},{4,11},{5,12},{6,13},{7,14},{8,15},{9,16}... | collective-permute-start | bytes 1769480
  650.8 81.3 %collective-permute-start.5 = (f32[24,6144]{1,0:T(8,128)S(1)}, f32[24,6144]{1,0:T(8,128)S(1)}, u32[]{:S(2)}, u32[]{:S(2)}) collective-permute-start(f32[24,6144]{1,0:T(8,128)S(1)} %get-tuple-element.70), channel_id=1, source_target_pairs={{0,6},{1,7},{2,8},{3,9},{4,10},{5,11},{6,12},{7,13},{8,14},{9,15},... | collective-permute-start | bytes 1769480
  657.1 5.9 collective-permute-start.15
  659.4 32.1 %collective-permute-start.13 = (f32[24,1536]{1,0:T(8,128)S(1)}, f32[24,1536]{1,0:T(8,128)S(1)}, u32[]{:S(2)}, u32[]{:S(2)}) collective-permute-start(f32[24,1536]{1,0:T(8,128)S(1)} %get-tuple-element.71), channel_id=1, source_target_pairs={{0,6},{1,7},{2,8},{3,9},{4,10},{5,11},{6,12},{7,13},{8,14},{9,15},... | collective-permute-start | bytes 442376
  662.9 31.8 %collective-permute-start.12 = (f32[24,1536]{1,0:T(8,128)S(1)}, f32[24,1536]{1,0:T(8,128)S(1)}, u32[]{:S(2)}, u32[]{:S(2)}) collective-permute-start(f32[24,1536]{1,0:T(8,128)S(1)} %get-tuple-element.71), channel_id=1, source_target_pairs={{0,5},{1,6},{2,7},{3,8},{4,9},{5,10},{6,11},{7,12},{8,13},{9,14},{... | collective-permute-start | bytes 442376
  687.3 38.3 %collective-permute-start.7 = (f32[18,6144]{1,0:T(8,128)S(1)}, f32[18,6144]{1,0:T(8,128)S(1)}, u32[]{:S(2)}, u32[]{:S(2)}) collective-permute-start(f32[18,6144]{1,0:T(8,128)S(1)} %slice), channel_id=1, source_target_pairs={{0,8},{1,9},{2,10},{3,11},{4,12},{5,13},{6,14},{7,15},{8,16},{9,17... | collective-permute-start | bytes 1327112
  691.5 16.6 %collective-permute-start.11 = (f32[24,1536]{1,0:T(8,128)S(1)}, f32[24,1536]{1,0:T(8,128)S(1)}, u32[]{:S(2)}, u32[]{:S(2)}) collective-permute-start(f32[24,1536]{1,0:T(8,128)S(1)} %get-tuple-element.71), channel_id=1, source_target_pairs={{0,4},{1,5},{2,6},{3,7},{4,8},{5,9},{6,10},{7,11},{8,12},{9,13},{1... | collective-permute-start | bytes 442376
  694.8 18.8 %collective-permute-start.10 = (f32[24,1536]{1,0:T(8,128)S(1)}, f32[24,1536]{1,0:T(8,128)S(1)}, u32[]{:S(2)}, u32[]{:S(2)}) collective-permute-start(f32[24,1536]{1,0:T(8,128)S(1)} %get-tuple-element.71), channel_id=1, source_target_pairs={{0,3},{1,4},{2,5},{3,6},{4,7},{5,8},{6,9},{7,10},{8,11},{9,12},{10... | collective-permute-start | bytes 442376
  708.1 9.3 collective-permute-start.9
  713.6 6.9 collective-permute-start.8
  717.4 25.9 %collective-permute-start.4 = (f32[24,6144]{1,0:T(8,128)S(1)}, f32[24,6144]{1,0:T(8,128)}, u32[]{:S(2)}, u32[]{:S(2)}) collective-permute-start(f32[24,6144]{1,0:T(8,128)S(1)} %get-tuple-element.70), channel_id=1, source_target_pairs={{0,5},{1,6},{2,7},{3,8},{4,9},{5,10},{6,11},{7,12},{8,13},{9,14},{... | collective-permute-start | bytes 1769480
  720.5 43.4 %collective-permute-start.3 = (f32[24,6144]{1,0:T(8,128)S(1)}, f32[24,6144]{1,0:T(8,128)}, u32[]{:S(2)}, u32[]{:S(2)}) collective-permute-start(f32[24,6144]{1,0:T(8,128)S(1)} %get-tuple-element.70), channel_id=1, source_target_pairs={{0,4},{1,5},{2,6},{3,7},{4,8},{5,9},{6,10},{7,11},{8,12},{9,13},{1... | collective-permute-start | bytes 1769480
  725.7 45.7 %collective-permute-start.2 = (f32[24,6144]{1,0:T(8,128)S(1)}, f32[24,6144]{1,0:T(8,128)S(1)}, u32[]{:S(2)}, u32[]{:S(2)}) collective-permute-start(f32[24,6144]{1,0:T(8,128)S(1)} %get-tuple-element.70), channel_id=1, source_target_pairs={{0,3},{1,4},{2,5},{3,6},{4,7},{5,8},{6,9},{7,10},{8,11},{9,12},{10... | collective-permute-start | bytes 1769480
  730.2 44.0 %collective-permute-start.1 = (f32[24,6144]{1,0:T(8,128)S(1)}, f32[24,6144]{1,0:T(8,128)}, u32[]{:S(2)}, u32[]{:S(2)}) collective-permute-start(f32[24,6144]{1,0:T(8,128)S(1)} %get-tuple-element.70), channel_id=1, source_target_pairs={{0,2},{1,3},{2,4},{3,5},{4,6},{5,7},{6,8},{7,9},{8,10},{9,11},{10,... | collective-permute-start | bytes 1769480
  732.1 42.0 %collective-permute-start = (f32[24,6144]{1,0:T(8,128)S(1)}, f32[24,6144]{1,0:T(8,128)}, u32[]{:S(2)}, u32[]{:S(2)}) collective-permute-start(f32[24,6144]{1,0:T(8,128)S(1)} %get-tuple-element.70), channel_id=1, source_target_pairs={{0,1},{1,2},{2,3},{3,4},{4,5},{5,6},{6,7},{7,8},{8,9},{9,10},{10,1... | collective-permute-start | bytes 1769480
  866.0 115.0 %all-gather.9.cloned.1.call-start = ((), (), s32[]{:S(2)}) async-start(), calls=%async_computation.5 | async-start | bytes 2027520 | tf_op jit(solution)/shard_map/all_gather | solution.py:65
  867.8 197.9 %all-gather.11.cloned.1.call-start = ((), (), s32[]{:S(2)}) async-start(), calls=%async_computation.6 | async-start | bytes 9732096 | tf_op jit(solution)/shard_map/all_gather | solution.py:65
  871.1 272.1 %all-gather.7.cloned.1.call-start = ((), (), s32[]{:S(2)}) async-start(), calls=%async_computation.4 | async-start | bytes 8110080 | tf_op jit(solution)/shard_map/all_gather | solution.py:65
  (18 other events, 1057.6 us)
Sparse Core Ops, SparseCore 0:
  153.7 104.0 reduce-scatter.8
  263.9 209.0 reduce-scatter.6
  866.1 57.3 all-gather.12
  926.3 54.6 all-gather.8
  984.3 81.3 all-gather.10
  1069.1 74.0 all-gather.6
where the time goes:
time: 1170 us; the launch traced here: 1160 us
  matrix products  368 us (31%)
  blocking collectives  306 us (26%)
  waiting for transfers between devices  298 us (25%)
  local copies, waits for them, and re-layouts  79.4 us (7%)
  starting transfers between devices  75.4 us (6%)
  between operations  20.6 us (2%)
  other arithmetic  14.5 us (1%)
    unnamed x1, blocking collectives  260 us
    all_gather x4, waiting for transfers between devices, per_device(): lax.all_gather(result[0].astype(jnp.bfloat16), 'dp', axis=0, tiled=True)  252 us
    unnamed x48, local copies, waits for them, and re-layouts  79.4 us
    unnamed x16, starting transfers between devices  75.2 us
    dot_general x1, matrix products, local_grads(): jnp.einsum('rd,rw->dw', x_rows, dz_one, preferred_element_type=jnp.float32)  70.9 us
    dot_general x1, matrix products, local_grads(): jnp.dot(x_rows, w_one, preferred_element_type=jnp.float32)  62 us
    dot_general x1, matrix products, local_grads(): jnp.einsum('rw,rd->wd', a_one, dh_two, preferred_element_type=jnp.float32)  58.5 us
    dot_general x1, matrix products, local_grads(): jnp.dot(a_one, w_two, preferred_element_type=jnp.float32)  52.4 us
  transfers between devices with their start and end apart: 22, of which 11 were waited for; matrix products, arithmetic and copies ran while one was open for 48% of the time, Pallas kernels for 0%

commit v1 on v0

v1 whole, which is shorter than its diff:
```python
import functools
import jax
import jax.numpy as jnp
from jax import lax
from jax.experimental import pallas as pl
from jax.experimental.pallas import tpu as pltpu
from jax.sharding import PartitionSpec as P

ADAM_STEP = 10
BETA_ONE = 0.9
BETA_TWO = 0.95
ADAM_EPS = 1e-8
NORM_EPS = 1e-6
BIAS_ONE = 1.0 - BETA_ONE ** ADAM_STEP
BIAS_TWO = 1.0 - BETA_TWO ** ADAM_STEP
INV_SQRT2 = 0.7071067811865476
INV_SQRT2PI = 0.3989422804014327
DP_SIZE = 32
MESH_ID = pl.DeviceIdType.MESH
W1_ROWS = 48 * 18
W3_ROWS = 12 * 18
PACK_ROWS = 1088
CHUNKS = 12
CHUNK_W = 512
ROWS_DEV = 4096
TILE_R = 512
LANES = 128
MODEL_DIM = 576
GROUP_ROWS = 72
HALF_ROWS = 288
OWN_ROWS = 18
Z_SIZE = 4
PAIR = 2
Z_PEERS = 3
PAD_ROWS = 24
WIDE_DIM = 6144
FF_DIM = 1536
STACK_ROWS = 240
TALL_ROWS = 192
SHORT_ROWS = 48


def gelu_value(pre_act):
    pre_wide = pre_act.astype(jnp.float32)
    return 0.5 * pre_wide * (1.0 + lax.erf(pre_wide * INV_SQRT2))


def device_of(core, x_pos, y_pos, z_pos):
    return ((z_pos * PAIR + y_pos) * PAIR + x_pos) * PAIR + core


def update_kernel(g1, g2, g3, g4, p1, p2, p3, p4, m1, m2, m3, m4, v1, v2, v3, v4, lr_ref, clip_ref,
                  all_p, all_q, p1n, p2n, p3n, p4n, m1n, m2n, m3n, m4n, v1n, v2n, v3n, v4n, norm_ref,
                  wide_p, own_p, own_q, norm_send, norm_recv,
                  norm_ssem, norm_rsem, send_p, recv_p, send_q, recv_q, local_sem):
    me = lax.axis_index('dp')
    core = me % PAIR
    x_pos = (me // PAIR) % PAIR
    y_pos = (me // Z_SIZE) % PAIR
    z_pos = me // 8
    core_peer = device_of(1 - core, x_pos, y_pos, z_pos)
    x_peer = device_of(core, 1 - x_pos, y_pos, z_pos)
    y_peer = device_of(core, x_pos, 1 - y_pos, z_pos)
    z_others = [(z_pos + k) % Z_SIZE for k in (1, PAIR, Z_PEERS)]
    z_peers = [device_of(core, x_pos, y_pos, zo) for zo in z_others]

    barrier = pltpu.get_barrier_semaphore()
    for peer in [core_peer, x_peer, y_peer] + z_peers:
        pl.semaphore_signal(barrier, inc=1, device_id=(peer,), device_id_type=MESH_ID)
    pl.semaphore_wait(barrier, 6)

    inv_dp = 1.0 / DP_SIZE
    total = jnp.zeros((1, LANES), jnp.float32)
    for g_ref in (g1, g3):
        for j in range(g_ref.shape[1] // LANES):
            g_val = g_ref[:, j * LANES:(j + 1) * LANES] * inv_dp
            total = total + jnp.sum(g_val * g_val, axis=0, keepdims=True)
    scal = jnp.sum(total)
    for g_ref in (g2, g4):
        g_val = g_ref[...] * inv_dp
        scal = scal + jnp.sum(g_val * g_val)
    part = jnp.full((8, LANES), scal, jnp.float32)
    for stage, peer in enumerate((core_peer, x_peer, y_peer)):
        norm_send[stage] = part
        copy = pltpu.make_async_remote_copy(src_ref=norm_send.at[stage], dst_ref=norm_recv.at[stage], send_sem=norm_ssem.at[stage], recv_sem=norm_rsem.at[stage], device_id=(peer,), device_id_type=MESH_ID)
        copy.start()
        copy.wait()
        part = part + norm_recv[stage]
    norm_send[Z_PEERS] = part
    norm_recv[Z_PEERS + z_pos] = part
    z_copies = []
    for k in range(Z_PEERS):
        z_copies.append(pltpu.make_async_remote_copy(src_ref=norm_send.at[Z_PEERS], dst_ref=norm_recv.at[Z_PEERS + z_pos], send_sem=norm_ssem.at[Z_PEERS + k], recv_sem=norm_rsem.at[Z_PEERS + z_pos], device_id=(z_peers[k],), device_id_type=MESH_ID))
        z_copies[-1].start()
    for k in range(Z_PEERS):
        pltpu.make_async_remote_copy(src_ref=norm_send.at[Z_PEERS], dst_ref=norm_recv.at[Z_PEERS + z_others[k]], send_sem=norm_ssem.at[Z_PEERS + k], recv_sem=norm_rsem.at[Z_PEERS + z_others[k]], device_id=(z_peers[k],), device_id_type=MESH_ID).wait_recv()
    for k in range(Z_PEERS):
        z_copies[k].wait_send()
    sq_all = ((norm_recv[Z_PEERS] + norm_recv[Z_SIZE]) + norm_recv[5]) + norm_recv[6]
    norm_val = jnp.sqrt(sq_all)
    norm_ref[...] = norm_val
    lr_val = lr_ref[0, 0]
    scale = jnp.minimum(1.0, clip_ref[0, 0] / (norm_val + NORM_EPS))[0:1, :]

    def adam(g_val, p_val, m_val, v_val, s_val):
        scaled = s_val * (g_val * inv_dp)
        mom_new = BETA_ONE * m_val + (1.0 - BETA_ONE) * scaled
        var_new = BETA_TWO * v_val + (1.0 - BETA_TWO) * scaled * scaled
        return p_val - lr_val * (mom_new / BIAS_ONE) / (jnp.sqrt(var_new / BIAS_TWO) + ADAM_EPS), mom_new, var_new

    for base, (g_ref, p_ref, m_ref, v_ref, pn, mn, vn) in ((0, (g1, p1, m1, v1, p1n, m1n, v1n)), (W1_ROWS, (g3, p3, m3, v3, p3n, m3n, v3n))):
        for j in range(g_ref.shape[1] // LANES):
            cols = slice(j * LANES, (j + 1) * LANES)
            p_new, m_new, v_new = adam(g_ref[:, cols], p_ref[:, cols], m_ref[:, cols], v_ref[:, cols], scale)
            pn[:, cols] = p_new
            mn[:, cols] = m_new
            vn[:, cols] = v_new
            wide_p[base + OWN_ROWS * j:base + OWN_ROWS * (j + 1), :] = p_new
    wide_p[W1_ROWS + W3_ROWS:, :] = jnp.zeros((PACK_ROWS - W1_ROWS - W3_ROWS, LANES), jnp.float32)
    own_p[...] = wide_p[...].astype(jnp.bfloat16)
    scale_one = scale[0:1, 0:1]
    for base, (g_ref, p_ref, m_ref, v_ref, pn, mn, vn) in ((0, (g2, p2, m2, v2, p2n, m2n, v2n)), (TALL_ROWS, (g4, p4, m4, v4, p4n, m4n, v4n))):
        for r in range(g_ref.shape[0] // 16):
            rows = slice(r * 16, (r + 1) * 16)
            p_new, m_new, v_new = adam(g_ref[rows, :], p_ref[rows, :], m_ref[rows, :], v_ref[rows, :], scale_one)
            pn[rows, :] = p_new
            mn[rows, :] = m_new
            vn[rows, :] = v_new
            own_q[base + 16 * r:base + 16 * (r + 1), :] = p_new.astype(jnp.bfloat16)

    loc_p = pltpu.make_async_copy(own_p, all_p.at[me], local_sem.at[0])
    loc_q = pltpu.make_async_copy(own_q, all_q.at[me], local_sem.at[1])
    loc_p.start()
    loc_q.start()

    pending = []

    def send(buf, own, ssem, rsem, kind, slot, origin, peer, first):
        src = own if first else buf.at[origin]
        copy = pltpu.make_async_remote_copy(src_ref=src, dst_ref=buf.at[origin], send_sem=ssem.at[kind, slot], recv_sem=rsem.at[origin], device_id=(peer,), device_id_type=MESH_ID)
        copy.start()
        pending.append(copy)

    def arrive(buf, own, ssem, rsem, origin):
        pltpu.make_async_remote_copy(src_ref=own, dst_ref=buf.at[origin], send_sem=ssem.at[0, 0], recv_sem=rsem.at[origin], device_id=(core_peer,), device_id_type=MESH_ID).wait_recv()

    sets = ((all_p, own_p, send_p, recv_p, y_peer, x_peer, True), (all_q, own_q, send_q, recv_q, x_peer, y_peer, False))

    def origin_of(y_first, dz, da, db, dc=0):
        zo = (z_pos + dz) % Z_SIZE
        yo, xo = (da, db) if y_first else (db, da)
        return device_of((core + dc) % PAIR, (x_pos + xo) % PAIR, (y_pos + yo) % PAIR, zo)

    for buf, own, ssem, rsem, peer_a, peer_b, y_first in sets:
        send(buf, own, ssem, rsem, Z_PEERS, 0, me, peer_a, True)
        send(buf, own, ssem, rsem, Z_SIZE, 0, me, peer_b, True)
        for k in range(Z_PEERS):
            send(buf, own, ssem, rsem, k, 0, me, z_peers[k], True)
        send(buf, own, ssem, rsem, 5, 0, me, core_peer, True)
    steps = [(0, 1, 0)]
    for dz in (1, Z_PEERS, PAIR):
        steps += [(dz, 0, 0)]
    for dz in (1, Z_PEERS, PAIR):
        steps += [(dz, 1, 0)]
    for dz, da, _ in steps:
        for buf, own, ssem, rsem, peer_a, peer_b, y_first in sets:
            origin = origin_of(y_first, dz, da, 0)
            arrive(buf, own, ssem, rsem, origin)
            slot = dz * PAIR + da
            if da == 0:
                send(buf, own, ssem, rsem, Z_PEERS, dz, origin, peer_a, False)
            send(buf, own, ssem, rsem, Z_SIZE, slot, origin, peer_b, False)
            send(buf, own, ssem, rsem, 5, slot, origin, core_peer, False)
    for dz, da in [(0, 0), (0, 1), (1, 0), (Z_PEERS, 0), (PAIR, 0), (1, 1), (Z_PEERS, 1), (PAIR, 1)]:
        for buf, own, ssem, rsem, peer_a, peer_b, y_first in sets:
            origin = origin_of(y_first, dz, da, 1)
            arrive(buf, own, ssem, rsem, origin)
            send(buf, own, ssem, rsem, 5, 8 + dz * PAIR + da, origin, core_peer, False)
    for dz in range(Z_SIZE):
        for da in range(PAIR):
            for db in range(PAIR):
                for buf, own, ssem, rsem, peer_a, peer_b, y_first in sets:
                    arrive(buf, own, ssem, rsem, origin_of(y_first, dz, da, db, 1))
    for copy in pending:
        copy.wait_send()
    loc_p.wait()
    loc_q.wait()


def update_call(grads, masters, moms, variances, learn_rate, clip_max):
    f32 = jnp.float32
    bf16 = jnp.bfloat16
    vmem = pl.BlockSpec(memory_space=pltpu.VMEM)
    smem = pl.BlockSpec(memory_space=pltpu.SMEM)
    hbm = pl.BlockSpec(memory_space=pl.ANY)
    shapes = [jax.ShapeDtypeStruct(a.shape, f32) for a in masters]
    out_shape = [jax.ShapeDtypeStruct((DP_SIZE, PACK_ROWS, LANES), bf16), jax.ShapeDtypeStruct((DP_SIZE, STACK_ROWS, MODEL_DIM), bf16)] + shapes * Z_PEERS + [jax.ShapeDtypeStruct((8, LANES), f32)]
    return pl.pallas_call(
        update_kernel,
        out_shape=out_shape,
        in_specs=[vmem] * 16 + [smem] * PAIR,
        out_specs=[hbm, hbm] + [vmem] * 13,
        scratch_shapes=[
            pltpu.VMEM((PACK_ROWS, LANES), f32),
            pltpu.VMEM((PACK_ROWS, LANES), bf16),
            pltpu.VMEM((STACK_ROWS, MODEL_DIM), bf16),
            pltpu.VMEM((Z_SIZE, 8, LANES), f32),
            pltpu.VMEM((7, 8, LANES), f32),
            pltpu.SemaphoreType.DMA((6,)),
            pltpu.SemaphoreType.DMA((7,)),
            pltpu.SemaphoreType.DMA((6, 16)),
            pltpu.SemaphoreType.DMA((DP_SIZE,)),
            pltpu.SemaphoreType.DMA((6, 16)),
            pltpu.SemaphoreType.DMA((DP_SIZE,)),
            pltpu.SemaphoreType.DMA((PAIR,)),
        ],
        compiler_params=pltpu.CompilerParams(collective_id=0, has_side_effects=True, vmem_limit_bytes=40 * 1024 * 1024),
        name='adam_gather',
    )(*grads, *masters, *moms, *variances, learn_rate.reshape(1, 1), clip_max.reshape(1, 1))


def scatter_kernel(z_hbm, dh_hbm, dht_hbm, xt_hbm, w2_hbm, out1, out2,
                   dh, dht, xt, zbuf, w2c, a_even, a_odd, d_even, d_odd, acc1, acc2,
                   ra0, ra1, ra2, ra3, rb0, rb1, rb2, rb3, s1a, s2a, s3a, s1b, s2b, s3b, own2, qbuf,
                   in_sem, zsem, wsem, sa_send, sa_recv, sb_send, sb_recv, za_send, za_recv, zb_send, zb_recv, ga_send, ga_recv, fix_send, fix_recv):
    f32 = jnp.float32
    me = lax.axis_index('dp')
    core = me % PAIR
    x_pos = (me // PAIR) % PAIR
    y_pos = (me // Z_SIZE) % PAIR
    z_pos = me // 8
    core_peer = device_of(1 - core, x_pos, y_pos, z_pos)
    x_peer = device_of(core, 1 - x_pos, y_pos, z_pos)
    y_peer = device_of(core, x_pos, 1 - y_pos, z_pos)
    diag_peer = device_of(1 - core, 1 - x_pos, y_pos, z_pos)
    z_others = [(z_pos + k) % Z_SIZE for k in (1, PAIR, Z_PEERS)]
    z_peers = [device_of(core, x_pos, y_pos, zo) for zo in z_others]

    big = [pltpu.make_async_copy(src, dst, in_sem.at[i]) for i, (src, dst) in enumerate(((dh_hbm, dh), (dht_hbm, dht), (xt_hbm, xt)))]

    def chunk_copies(chunk):
        slot = chunk % PAIR
        zt = chunk % Z_SIZE
        k = chunk // Z_SIZE
        copies = []
        for b in range(Z_SIZE):
            off = pl.multiple_of(384 * (Z_SIZE * zt + b) + LANES * k, LANES)
            copies.append(pltpu.make_async_copy(z_hbm.at[:, pl.ds(off, LANES)], zbuf.at[slot, b], zsem.at[slot, b]))
            copies.append(pltpu.make_async_copy(w2_hbm.at[pl.ds(off, LANES), :], w2c.at[slot, pl.ds(b * LANES, LANES), :], wsem.at[slot, b]))
        return copies

    big[0].start()
    for copy in chunk_copies(0):
        copy.start()
    big[1].start()
    big[PAIR].start()
    qbuf[...] = jnp.zeros(qbuf.shape, f32)

    barrier = pltpu.get_barrier_semaphore()
    for peer in [core_peer, x_peer, y_peer, diag_peer] + z_peers:
        pl.semaphore_signal(barrier, inc=1, device_id=(peer,), device_id_type=MESH_ID)
    pl.semaphore_wait(barrier, 7)
    for copy in big:
        copy.wait()

    def remote(src, dst, ssem, rsem, peer):
        return pltpu.make_async_remote_copy(src_ref=src, dst_ref=dst, send_sem=ssem, recv_sem=rsem, device_id=(peer,), device_id_type=MESH_ID)

    def pair0(chunk):
        slot = chunk % PAIR
        return (remote(acc1.at[slot, 1 - core], ra0.at[slot], sa_send.at[0], sa_recv.at[0, slot], core_peer),
                remote(acc2.at[slot, :, :, 1 - core], rb0.at[slot], sb_send.at[0], sb_recv.at[0, slot], core_peer))

    def pair1(chunk):
        slot = chunk % PAIR
        return (remote(s1a.at[:, :, 1 - y_pos], ra1.at[slot], sa_send.at[1], sa_recv.at[1, slot], y_peer),
                remote(s1b.at[:, 1 - x_pos], rb1.at[slot], sb_send.at[1], sb_recv.at[1, slot], x_peer))

    def pair2(chunk):
        slot = chunk % PAIR
        return (remote(s2a.at[1 - x_pos], ra2.at[slot], sa_send.at[PAIR], sa_recv.at[PAIR, slot], x_peer),
                remote(s2b.at[1 - y_pos], rb2.at[slot], sb_send.at[PAIR], sb_recv.at[PAIR, slot], y_peer))

    def z_send_a(chunk):
        slot = chunk % PAIR
        return [remote(s3a.at[z_others[k]], ra3.at[slot, z_pos], za_send.at[k], za_recv.at[slot, z_pos], z_peers[k]) for k in range(Z_PEERS)]

    def z_recv_a(chunk):
        slot = chunk % PAIR
        return [remote(s3a.at[z_others[k]], ra3.at[slot, z_others[k]], za_send.at[k], za_recv.at[slot, z_others[k]], z_peers[k]) for k in range(Z_PEERS)]

    def z_send_b(chunk):
        zt = chunk % Z_SIZE
        return remote(s3b, rb3.at[chunk // Z_SIZE, z_pos], zb_send.at[0], zb_recv.at[chunk // Z_SIZE, z_pos], device_of(core, x_pos, y_pos, zt))

    def z_recv_b(chunk):
        return [remote(s3b, rb3.at[chunk // Z_SIZE, z_others[k]], zb_send.at[0], zb_recv.at[chunk // Z_SIZE, z_others[k]], z_peers[k]) for k in range(Z_PEERS)]

    lane_me = core * PAIR + x_pos
    group = ((1 - core, x_pos, core_peer), (core, 1 - x_pos, x_peer), (1 - core, 1 - x_pos, diag_peer))

    def g_send(chunk):
        slot = chunk % PAIR
        return [remote(qbuf.at[gx * PAIR + gc], out1.at[lane_me, chunk], ga_send.at[i], ga_recv.at[i, slot], peer) for i, (gc, gx, peer) in enumerate(group)]

    def g_recv(chunk):
        slot = chunk % PAIR
        return [remote(qbuf.at[gx * PAIR + gc], out1.at[gc * PAIR + gx, chunk], ga_send.at[i], ga_recv.at[i, slot], peer) for i, (gc, gx, peer) in enumerate(group)]

    def within(t, lead):
        return jnp.logical_and(t >= lead, t < lead + CHUNKS)

    def elementwise(slot, r, a_buf, d_buf):
        rows = pl.ds(pl.multiple_of(r * TILE_R, TILE_R), TILE_R)
        back = lax.dot_general(dh[rows, :], w2c[slot], (((1,), (1,)), ((), ())), preferred_element_type=f32).astype(jnp.bfloat16)
        for b in range(Z_SIZE):
            cols = slice(b * LANES, (b + 1) * LANES)
            wide = zbuf[slot, b, rows, :].astype(f32)
            cdf = 0.5 * (1.0 + lax.erf(wide * INV_SQRT2))
            a_buf[:, cols] = (wide * cdf).astype(jnp.bfloat16)
            slope = cdf + wide * INV_SQRT2PI * jnp.exp(-0.5 * wide * wide)
            d_buf[:, cols] = (back[:, cols].astype(f32) * slope).astype(jnp.bfloat16)

    def accumulate(slot, r, a_buf, d_buf, first):
        rows = pl.ds(pl.multiple_of(r * TILE_R, TILE_R), TILE_R)
        part1 = jnp.dot(xt[:, rows], d_buf[...], preferred_element_type=f32)
        part2 = jnp.dot(dht[:, rows], a_buf[...], preferred_element_type=f32)
        for b in range(Z_SIZE):
            c1, x1 = b // PAIR, b % PAIR
            val1 = part1[:, b * LANES:(b + 1) * LANES].reshape(Z_SIZE, PAIR, GROUP_ROWS, LANES)
            val2 = part2[:, b * LANES:(b + 1) * LANES].reshape(PAIR, HALF_ROWS, LANES)
            if first:
                acc1[slot, c1, x1] = val1
                acc2[slot, b // PAIR, b % PAIR] = val2
            else:
                acc1[slot, c1, x1] = acc1[slot, c1, x1] + val1
                acc2[slot, b // PAIR, b % PAIR] = acc2[slot, b // PAIR, b % PAIR] + val2

    n_tiles = ROWS_DEV // TILE_R

    def compute(chunk):
        slot = chunk % PAIR
        for copy in chunk_copies(chunk):
            copy.wait()

        @pl.when(chunk + 1 < CHUNKS)
        def _():
            for copy in chunk_copies(chunk + 1):
                copy.start()

        elementwise(slot, 0, a_even, d_even)
        elementwise(slot, 1, a_odd, d_odd)
        accumulate(slot, 0, a_even, d_even, True)

        def body(i, carry):
            elementwise(slot, PAIR * i, a_even, d_even)
            accumulate(slot, PAIR * i - 1, a_odd, d_odd, False)
            elementwise(slot, PAIR * i + 1, a_odd, d_odd)
            accumulate(slot, PAIR * i, a_even, d_even, False)
            return carry

        lax.fori_loop(1, n_tiles // PAIR, body, 0)
        accumulate(slot, n_tiles - 1, a_odd, d_odd, False)

    def step(t, carry):
        @pl.when(within(t, 6))
        def _():
            for copy in g_send(t - 6):
                copy.wait_send()
            for copy in g_recv(t - 6):
                copy.wait_recv()

        @pl.when(within(t, 5))
        def _():
            chunk = t - 5
            slot = chunk % PAIR
            zt = chunk % Z_SIZE
            for copy in z_send_a(chunk):
                copy.wait_send()
            for copy in z_recv_a(chunk):
                copy.wait_recv()
            full = s3a[z_pos] + ra3[slot, z_others[0]] + ra3[slot, z_others[1]] + ra3[slot, z_others[PAIR]]
            for o in range(Z_SIZE):
                qbuf[o, 0:OWN_ROWS, :] = full[OWN_ROWS * o:OWN_ROWS * (o + 1), :]
            out1[lane_me, chunk] = qbuf[x_pos * PAIR + core]

            @pl.when(z_pos == zt)
            def _():
                for copy in z_recv_b(chunk):
                    copy.wait_recv()
                k = chunk // Z_SIZE
                own2[k] = s3b[...] + rb3[k, z_others[0]] + rb3[k, z_others[1]] + rb3[k, z_others[PAIR]]

            @pl.when(z_pos != zt)
            def _():
                z_send_b(chunk).wait_send()

        @pl.when(within(t, Z_SIZE))
        def _():
            chunk = t - Z_SIZE
            slot = chunk % PAIR
            for copy in pair2(chunk):
                copy.wait()
            for z in range(Z_SIZE):
                s3a[z] = s2a[x_pos, z] + ra2[slot, z]
            s3b[...] = s2b[y_pos] + rb2[slot]

        @pl.when(within(t, Z_PEERS))
        def _():
            chunk = t - Z_PEERS
            slot = chunk % PAIR
            for copy in pair1(chunk):
                copy.wait()
            for x in range(PAIR):
                for z in range(Z_SIZE):
                    s2a[x, z] = s1a[x, z, y_pos] + ra1[slot, x, z]
            for y in range(PAIR):
                s2b[y] = s1b[y, x_pos] + rb1[slot, y]

        @pl.when(within(t, PAIR))
        def _():
            chunk = t - PAIR
            slot = chunk % PAIR
            for copy in pair0(chunk):
                copy.wait()
            for x in range(PAIR):
                s1a[x] = acc1[slot, core, x] + ra0[slot, x]
            for y in range(PAIR):
                for x in range(PAIR):
                    s1b[y, x] = acc2[slot, y, x, core] + rb0[slot, y, x]

        @pl.when(within(t, 1))
        def _():
            for copy in pair0(t - 1):
                copy.start()

        @pl.when(within(t, PAIR))
        def _():
            for copy in pair1(t - PAIR):
                copy.start()

        @pl.when(within(t, Z_PEERS))
        def _():
            for copy in pair2(t - Z_PEERS):
                copy.start()

        @pl.when(within(t, Z_SIZE))
        def _():
            chunk = t - Z_SIZE
            for copy in z_send_a(chunk):
                copy.start()

            @pl.when(z_pos != chunk % Z_SIZE)
            def _():
                z_send_b(chunk).start()

        @pl.when(within(t, 5))
        def _():
            for copy in g_send(t - 5):
                copy.start()

        @pl.when(t < CHUNKS)
        def _():
            compute(t)

        return carry

    lax.fori_loop(0, CHUNKS + 6, step, 0)

    fixes = [remote(own2.at[1 - core + i], out2.at[i, core], fix_send.at[i], fix_recv.at[i], core_peer) for i in range(PAIR)]
    for copy in fixes:
        copy.start()
    for i in range(PAIR):
        out2[i, core] = own2[core + i]
    for i in range(PAIR):
        remote(own2.at[1 - core + i], out2.at[i, 1 - core], fix_send.at[i], fix_recv.at[i], core_peer).wait()


def scatter_call(z_one, dh_two, dh_two_t, x_t, w_two):
    f32 = jnp.float32
    bf16 = jnp.bfloat16
    hbm = pl.BlockSpec(memory_space=pl.ANY)
    vmem = pl.BlockSpec(memory_space=pltpu.VMEM)
    dma = pltpu.SemaphoreType.DMA
    buf = pltpu.VMEM
    return pl.pallas_call(
        scatter_kernel,
        out_shape=[jax.ShapeDtypeStruct((Z_SIZE, CHUNKS, PAD_ROWS, LANES), f32), jax.ShapeDtypeStruct((PAIR, PAIR, HALF_ROWS, LANES), f32)],
        in_specs=[hbm] * 5,
        out_specs=[vmem, vmem],
        scratch_shapes=[
            buf((ROWS_DEV, MODEL_DIM), bf16), buf((MODEL_DIM, ROWS_DEV), bf16), buf((MODEL_DIM, ROWS_DEV), bf16),
            buf((PAIR, Z_SIZE, ROWS_DEV, LANES), bf16), buf((PAIR, CHUNK_W, MODEL_DIM), bf16),
            buf((TILE_R, CHUNK_W), bf16), buf((TILE_R, CHUNK_W), bf16), buf((TILE_R, CHUNK_W), bf16), buf((TILE_R, CHUNK_W), bf16),
            buf((PAIR, PAIR, PAIR, Z_SIZE, PAIR, GROUP_ROWS, LANES), f32), buf((PAIR, PAIR, PAIR, PAIR, HALF_ROWS, LANES), f32),
            buf((PAIR, PAIR, Z_SIZE, PAIR, GROUP_ROWS, LANES), f32), buf((PAIR, PAIR, Z_SIZE, GROUP_ROWS, LANES), f32), buf((PAIR, Z_SIZE, GROUP_ROWS, LANES), f32), buf((PAIR, Z_SIZE, GROUP_ROWS, LANES), f32),
            buf((PAIR, PAIR, PAIR, HALF_ROWS, LANES), f32), buf((PAIR, PAIR, HALF_ROWS, LANES), f32), buf((PAIR, HALF_ROWS, LANES), f32), buf((Z_PEERS, Z_SIZE, HALF_ROWS, LANES), f32),
            buf((PAIR, Z_SIZE, PAIR, GROUP_ROWS, LANES), f32), buf((PAIR, Z_SIZE, GROUP_ROWS, LANES), f32), buf((Z_SIZE, GROUP_ROWS, LANES), f32),
            buf((PAIR, PAIR, HALF_ROWS, LANES), f32), buf((PAIR, HALF_ROWS, LANES), f32), buf((HALF_ROWS, LANES), f32),
            buf((Z_PEERS, HALF_ROWS, LANES), f32), buf((Z_SIZE, PAD_ROWS, LANES), f32),
            dma((Z_PEERS,)), dma((PAIR, Z_SIZE)), dma((PAIR, Z_SIZE)),
            dma((Z_PEERS,)), dma((Z_PEERS, PAIR)), dma((Z_PEERS,)), dma((Z_PEERS, PAIR)),
            dma((Z_PEERS,)), dma((PAIR, Z_SIZE)), dma((1,)), dma((Z_PEERS, Z_SIZE)),
            dma((Z_PEERS,)), dma((Z_PEERS, PAIR)), dma((PAIR,)), dma((PAIR,)),
        ],
        compiler_params=pltpu.CompilerParams(collective_id=1, has_side_effects=True, vmem_limit_bytes=60 * 1024 * 1024),
        cost_estimate=pl.CostEstimate(flops=100_000_000_000, bytes_accessed=80_000_000, transcendentals=50_000_000),
        name='grad_scatter',
    )(z_one, dh_two, dh_two_t, x_t, w_two)


def forward_kernel(x_ref, dy_ref, w1, w2, w3, w4, z_out, dh_out, dht_out, xt_out, g3_out, g4t_out,
                   h_acc, a_even, a_odd, h_t, dy_t):
    f32 = jnp.float32
    bf16 = jnp.bfloat16

    @pl.when(pl.program_id(0) == 0)
    def _():
        g3_out[...] = jnp.zeros(g3_out.shape, f32)
        g4t_out[...] = jnp.zeros(g4t_out.shape, f32)

    def hidden(c, a_buf):
        cols = pl.ds(pl.multiple_of(c * CHUNK_W, CHUNK_W), CHUNK_W)
        z_val = jnp.dot(x_ref[...], w1[:, cols], preferred_element_type=f32).astype(bf16)
        z_out[:, cols] = z_val
        a_buf[...] = gelu_value(z_val).astype(bf16)

    def project(c, a_buf, first):
        rows = pl.ds(pl.multiple_of(c * CHUNK_W, CHUNK_W), CHUNK_W)
        part = jnp.dot(a_buf[...], w2[rows, :], preferred_element_type=f32)
        if first:
            h_acc[...] = part
        else:
            h_acc[...] = h_acc[...] + part

    xt_out[...] = x_ref[...].T
    dy_t[...] = dy_ref[...].T
    hidden(0, a_even)
    hidden(1, a_odd)
    project(0, a_even, True)

    def body(i, carry):
        hidden(PAIR * i, a_even)
        project(PAIR * i - 1, a_odd, False)
        hidden(PAIR * i + 1, a_odd)
        project(PAIR * i, a_even, False)
        return carry

    lax.fori_loop(1, CHUNKS // PAIR, body, 0)
    project(CHUNKS - 1, a_odd, False)
    h_two = h_acc[...].astype(bf16)
    h_t[...] = h_two.T
    dh_sum = None
    for j in range(w3.shape[1] // CHUNK_W):
        cols = slice(j * CHUNK_W, (j + 1) * CHUNK_W)
        z_three = jnp.dot(h_two, w3[:, cols], preferred_element_type=f32).astype(bf16)
        wide = z_three.astype(f32)
        cdf = 0.5 * (1.0 + lax.erf(wide * INV_SQRT2))
        a_three = (wide * cdf).astype(bf16)
        slope = cdf + wide * INV_SQRT2PI * jnp.exp(-0.5 * wide * wide)
        da_three = lax.dot_general(dy_ref[...], w4[cols, :], (((1,), (1,)), ((), ())), preferred_element_type=f32).astype(bf16)
        dz_three = (da_three.astype(f32) * slope).astype(bf16)
        g4t_out[:, cols] = g4t_out[:, cols] + jnp.dot(dy_t[...], a_three, preferred_element_type=f32)
        g3_out[:, cols] = g3_out[:, cols] + jnp.dot(h_t[...], dz_three, preferred_element_type=f32)
        part = lax.dot_general(dz_three, w3[:, cols], (((1,), (1,)), ((), ())), preferred_element_type=f32)
        dh_sum = part if dh_sum is None else dh_sum + part
    dh_two = dh_sum.astype(bf16)
    dh_out[...] = dh_two
    dht_out[...] = dh_two.T


def forward_call(x_rows, dy_rows, w_one, w_two, w_three, w_four):
    f32 = jnp.float32
    bf16 = jnp.bfloat16
    buf = pltpu.VMEM
    rows_in = pl.BlockSpec((TILE_R, MODEL_DIM), lambda i: (i, 0))
    cols_out = pl.BlockSpec((MODEL_DIM, TILE_R), lambda i: (0, i))
    whole = lambda a: pl.BlockSpec(a.shape, lambda i: (0, 0), pipeline_mode=pl.Buffered(1))
    small = jax.ShapeDtypeStruct((MODEL_DIM, FF_DIM), f32)
    tall = jax.ShapeDtypeStruct((ROWS_DEV, MODEL_DIM), bf16)
    flat = jax.ShapeDtypeStruct((MODEL_DIM, ROWS_DEV), bf16)
    return pl.pallas_call(
        forward_kernel,
        grid=(ROWS_DEV // TILE_R,),
        out_shape=[jax.ShapeDtypeStruct((ROWS_DEV, WIDE_DIM), bf16), tall, flat, flat, small, small],
        in_specs=[rows_in, rows_in] + [whole(a) for a in (w_one, w_two, w_three, w_four)],
        out_specs=[pl.BlockSpec((TILE_R, WIDE_DIM), lambda i: (i, 0)), rows_in, cols_out, cols_out, whole(small), whole(small)],
        scratch_shapes=[buf((TILE_R, MODEL_DIM), f32), buf((TILE_R, CHUNK_W), bf16), buf((TILE_R, CHUNK_W), bf16), buf((MODEL_DIM, TILE_R), bf16), buf((MODEL_DIM, TILE_R), bf16)],
        compiler_params=pltpu.CompilerParams(vmem_limit_bytes=60 * 1024 * 1024),
        cost_estimate=pl.CostEstimate(flops=100_000_000_000, bytes_accessed=100_000_000, transcendentals=50_000_000),
        name='forward_chain',
    )(x_rows, dy_rows, w_one, w_two, w_three, w_four)


def unpack_kernel(p_ref, q_ref, w1_out, w2_out, w3_out, w4_out, wide, lane_buf):
    owners = p_ref.shape[0]
    for o in range(owners):
        wide[o] = p_ref[o].astype(jnp.float32)
        w2_out[o * TALL_ROWS:(o + 1) * TALL_ROWS, :] = q_ref[o, :TALL_ROWS, :]
        w4_out[o * SHORT_ROWS:(o + 1) * SHORT_ROWS, :] = q_ref[o, TALL_ROWS:, :]
    for w_out, base in ((w1_out, 0), (w3_out, W1_ROWS)):
        for j in range(w_out.shape[1] // LANES):
            for o in range(owners):
                lane_buf[j % PAIR, o * OWN_ROWS:(o + 1) * OWN_ROWS, :] = wide[o, base + j * OWN_ROWS:base + (j + 1) * OWN_ROWS, :]
            w_out[:, j * LANES:(j + 1) * LANES] = lane_buf[j % PAIR].astype(jnp.bfloat16)


def unpack_call(all_p, all_q):
    f32 = jnp.float32
    bf16 = jnp.bfloat16
    owners = 8
    shapes = ((MODEL_DIM, WIDE_DIM), (WIDE_DIM, MODEL_DIM), (MODEL_DIM, FF_DIM), (FF_DIM, MODEL_DIM))
    steps = DP_SIZE // owners
    return pl.pallas_call(
        unpack_kernel,
        grid=(steps,),
        out_shape=[jax.ShapeDtypeStruct(s, bf16) for s in shapes],
        in_specs=[pl.BlockSpec((owners, PACK_ROWS, LANES), lambda i: (i, 0, 0)), pl.BlockSpec((owners, STACK_ROWS, MODEL_DIM), lambda i: (i, 0, 0))],
        out_specs=[pl.BlockSpec((s[0] // steps, s[1]), lambda i: (i, 0)) for s in shapes],
        scratch_shapes=[pltpu.VMEM((owners, PACK_ROWS, LANES), f32), pltpu.VMEM((PAIR, owners * OWN_ROWS, LANES), f32)],
        compiler_params=pltpu.CompilerParams(vmem_limit_bytes=SHORT_ROWS * 1024 * 1024),
        name='unpack_weights',
    )(all_p, all_q)


def solution(mesh):
    row_spec = P('dp', None)
    rep_spec = P()

    def per_device(x_rows, dy_rows, w_one, w_two, w_three, w_four, master_one, master_two, master_three, master_four, m_one, m_two, m_three, m_four, v_one, v_two, v_three, v_four, learn_rate, clip_max):
        z_one, dh_two, dh_two_t, x_t, g_three, g_four_t = forward_call(x_rows, dy_rows, w_one, w_two, w_three, w_four)
        s_four = lax.psum_scatter(g_four_t.T, 'dp', scatter_dimension=0, tiled=True)
        s_three = lax.psum_scatter(g_three.reshape(-1, LANES), 'dp', scatter_dimension=0, tiled=True).reshape(OWN_ROWS, FF_DIM)
        sum_one, sum_two = scatter_call(z_one, dh_two, dh_two_t, x_t, w_two)
        s_one = sum_one.reshape(Z_SIZE, Z_PEERS, Z_SIZE, PAD_ROWS, LANES)[:, :, :, :OWN_ROWS].transpose(Z_PEERS, PAIR, 0, 1, Z_SIZE).reshape(OWN_ROWS, WIDE_DIM)
        flat_two = sum_two.transpose(1, PAIR, 0, Z_PEERS).reshape(MODEL_DIM, 256)
        s_two = lax.dynamic_slice_in_dim(flat_two, 64 * (lax.axis_index('dp') % PAIR), TALL_ROWS, axis=1).T
        outs = update_call((s_one, s_two, s_three, s_four), (master_one, master_two, master_three, master_four), (m_one, m_two, m_three, m_four), (v_one, v_two, v_three, v_four), learn_rate, clip_max)
        w1n, w2n, w3n, w4n = unpack_call(outs[0], outs[1])
        return (w1n, w2n, w3n, w4n) + tuple(outs[PAIR:14]) + (outs[14][0, 0],)

    in_specs = (row_spec, row_spec) + (rep_spec,) * Z_SIZE + (row_spec,) * 12 + (rep_spec, rep_spec)
    out_specs = (rep_spec,) * Z_SIZE + (row_spec,) * 12 + (rep_spec,)
    return jax.shard_map(per_device, mesh=mesh, in_specs=in_specs, out_specs=out_specs, check_vma=False)
```

time: 1170 us -> 621 us (0.53)
  Pallas kernels: 0 us -> 516 us
  matrix products: 368 us -> 0 us
  blocking collectives: 306 us -> 0 us
  waiting for transfers between devices: 298 us -> 0.07 us
  starting transfers between devices: 75.4 us -> 0.26 us
  other arithmetic: 14.5 us -> 0 us
    pallas_call x0 -> x4, Pallas kernels: none -> 516 us  [the longest x1 228 us: scatter_call(): pl.pallas_call(scatter_kernel, out_shape=[jax.ShapeDtypeStruct((Z_SIZE, C...]
    dot_general x10 -> x0, matrix products: 368 us -> none  [the longest x1 70.9 us: local_grads(): jnp.einsum('rd,rw->dw', x_rows, dz_one, preferred_element_type=jnp.float32)]
    unnamed x1 -> x0, blocking collectives: 260 us -> none
    all_gather x4 -> x0, waiting for transfers between devices: 252 us -> none  [per_device(): lax.all_gather(result[0].astype(jnp.bfloat16), 'dp', axis=0, tiled=True)]
    unnamed x16 -> x1, starting transfers between devices: 75.2 us -> 0.04 us
    unnamed x22 -> x3, waiting for transfers between devices: 46.1 us -> 0.05 us
    psum x1 -> x0, blocking collectives: 45.6 us -> none  [per_device(): grad_norm = jnp.sqrt(lax.psum(local_sq, 'dp'))]
    unnamed x48 -> x89, local copies, waits for them, and re-layouts: 79.4 us -> 72.3 us
  transfers between devices with their start and end apart: 22 -> 2, of which waited for: 11 -> 0; matrix products, arithmetic and copies ran while one was open for 48% -> 2% of each run, Pallas kernels for 0% -> 37%
where the time goes in v1:
time: 621 us; the launch traced here: 619 us
  Pallas kernels  516 us (83%)
  local copies, waits for them, and re-layouts  87.6 us (14%)
  between operations  15.6 us (3%)
    pallas_call x1, Pallas kernels, scatter_call(): pl.pallas_call(scatter_kernel, out_shape=[jax.ShapeDtypeStruct((Z_SIZE, C...  228 us
    pallas_call x1, Pallas kernels, forward_call(): pl.pallas_call(forward_kernel, grid=(ROWS_DEV // TILE_R,), out_shape=[jax...  150 us
    pallas_call x1, Pallas kernels, update_call(): pl.pallas_call(update_kernel, out_shape=out_shape, in_specs=[vmem] * 16 +...  125 us
    unnamed x89, local copies, waits for them, and re-layouts  72.3 us
  transfers between devices with their start and end apart: 2, of which 0 were waited for; matrix products, arithmetic and copies ran while one was open for 2% of the time, Pallas kernels for 37%

profile of v1, /device:TPU:9, one launch (start us, length us, event | category | flops | bytes accessed | tf_op | source)
XLA Modules:
  0.0 619.3 jit_solution(8227891755169225334)
XLA Ops:
  7.2 7.6 %copy.58.x_ref = bf16[4096,576]{1,0:T(8,128)(2,1)} copy(bf16[4096,576]{0,1:T(8,128)(2,1)} %param.20) | data formatting | bytes 9437184 | tf_op args[0]
  14.9 7.6 %copy.59.dy_ref = bf16[4096,576]{1,0:T(8,128)(2,1)} copy(bf16[4096,576]{0,1:T(8,128)(2,1)} %param.21) | data formatting | bytes 9437184 | tf_op args[1]
  22.5 10.6 %copy.60.w2.w2_hbm = bf16[6144,576]{1,0:T(8,128)(2,1)} copy(bf16[6144,576]{0,1:T(8,128)(2,1)} %param.23) | data formatting | bytes 14155776 | tf_op args[3]
  33.1 2.3 copy.61.w4
  35.4 150.3 %forward_chain.1 = (bf16[4096,6144]{1,0:T(8,128)(2,1)}, bf16[4096,576]{1,0:T(8,128)(2,1)}, bf16[576,4096]{1,0:T(8,128)(2,1)}, bf16[576,4096]{1,0:T(8,128)(2,1)},...) custom-call(bf16[4096,576]{1,0:T(8,128)(2,1)} %copy.58.x_ref, bf16[4096,576]{1,0:T(8,128)(2,1)} %copy.59.dy_ref, ...), custom_call_target="tpu_custom_call" | custom-call | flops 99999997952 | bytes 100000000 | tf_op jit(solution)/shard_map/forward_chain/pallas_call | solution.py:582
  185.7 4.9 reshape.58
  190.9 3.1 copy.66
  194.0 228.0 %grad_scatter.1 = (f32[4,12,24,128]{3,2,1,0:T(8,128)}, f32[2,2,288,128]{3,2,1,0:T(8,128)}) custom-call(bf16[4096,6144]{1,0:T(8,128)(2,1)} %get-tuple-element.44.z_hbm, bf16[4096,576]{1,0:T(8,128)(2,1)} %get-tuple-element.45.dh_hbm, bf16[576,4096]{1,0:T(8,128)(2,1)} %get-tuple-element.46.dht_hbm, bf16[576,4096]{1,0:T(8,128)(2,1)} %get-tuple-element.47.xt_hbm, ...), custom_call_target="tpu_custom_call" | custom-call | flops 99999997952 | bytes 80000000 | tf_op jit(solution)/shard_map/grad_scatter/pallas_call | solution.py:486
  422.1 1.5 copy.73
  423.9 2.1 copy.69
  425.9 2.5 reshape.62
  429.7 1.1 dynamic-slice_bitcast_fusion.g2
  430.8 0.9 reshape.59.g3
  431.8 1.0 copy-done.9
  432.8 1.0 copy-done.10
  433.9 0.9 copy-done.15
  440.2 125.4 %adam_gather.1 = (bf16[32,1088,128]{2,1,0:T(8,128)(2,1)}, bf16[32,240,576]{2,1,0:T(8,128)(2,1)}, f32[18,6144]{1,0:T(8,128)S(1)}, f32[192,576]{1,0:T(8,128)S(1)},...) custom-call(f32[18,6144]{1,0:T(8,128)S(1)} %reshape.56.g1, ...), custom_call_target="tpu_custom_call" | custom-call | tf_op jit(solution)/shard_map/adam_gather/pallas_call | solution.py:198
  574.3 12.1 %unpack_weights.1 = (bf16[576,6144]{1,0:T(8,128)(2,1)}, bf16[6144,576]{1,0:T(8,128)(2,1)}, bf16[576,1536]{1,0:T(8,128)(2,1)}, bf16[1536,576]{1,0:T(8,128)(2,1)S(1)}) custom-call(bf16[32,1088,128]{2,1,0:T(8,128)(2,1)} %get-tuple-element.52.p_ref, bf16[32,240,576]{2,1,0:T(8,128)(2,1)} %get-tuple-element.53.q_ref), custom_call_target="tpu_custom_call" | custom-call | tf_op jit(solution)/shard_map/unpack_weights/pallas_call | solution.py:614
  586.4 10.5 %copy.67 = bf16[6144,576]{0,1:T(8,128)(2,1)} copy(bf16[6144,576]{1,0:T(8,128)(2,1)} %get-tuple-element.106) | data formatting | bytes 14155776
  596.9 2.2 copy.68
  599.6 1.9 copy.88
  601.6 1.8 copy.89
  604.1 1.6 copy.91
  606.4 1.8 copy.93
  (83 shorter events, 21.0 us)
Async XLA Ops:
  7.2 423.6 %reduce-scatter.7.cloned.1.call-start = ((), (), s32[]{:S(2)}) async-start(), calls=%async_computation.3 | async-start | bytes 3649536
  22.5 10.6 %copy-start.34 = (bf16[1536,576]{0,1:T(8,128)(2,1)S(1)}, bf16[1536,576]{0,1:T(8,128)(2,1)}, u32[]{:S(2)}) copy-start(bf16[1536,576]{0,1:T(8,128)(2,1)} %param.25) | copy-start | bytes 5308420
  185.7 5.2 copy-start.33
  190.7 241.1 %reduce-scatter.5.cloned.1.call-start = ((), (), s32[]{:S(2)}) async-start(), calls=%async_computation.2 | async-start | bytes 4055040 | tf_op jit(solution)/shard_map/reduce_scatter | solution.py:632
  422.0 9.7 %copy-start = (f32[18,6144]{1,0:T(8,128)S(1)}, f32[18,6144]{1,0:T(8,128)}, u32[]{:S(2)}) copy-start(f32[18,6144]{1,0:T(8,128)} %p1.1) | copy-start | bytes 1327108
  422.1 9.7 %copy-start.1 = (f32[18,6144]{1,0:T(8,128)S(1)}, f32[18,6144]{1,0:T(8,128)}, u32[]{:S(2)}) copy-start(f32[18,6144]{1,0:T(8,128)} %m1.1) | copy-start | bytes 1327108
  422.1 9.7 %copy-start.2 = (f32[18,6144]{1,0:T(8,128)S(1)}, f32[18,6144]{1,0:T(8,128)}, u32[]{:S(2)}) copy-start(f32[18,6144]{1,0:T(8,128)} %v1.1) | copy-start | bytes 1327108
  422.1 9.7 %copy-start.8 = (f32[192,576]{1,0:T(8,128)S(1)}, f32[192,576]{1,0:T(8,128)}, u32[]{:S(2)}) copy-start(f32[192,576]{1,0:T(8,128)} %p2.1) | copy-start | bytes 1327108
  431.8 1.0 copy-start.9
  432.8 1.0 copy-start.10
  433.9 0.9 copy-start.15
  434.8 0.9 copy-start.16
  435.7 0.9 copy-start.17
  436.6 0.9 copy-start.24
  437.5 0.9 copy-start.25
  438.4 0.9 copy-start.26
  596.9 6.5 %copy-start.23 = (f32[18,1536]{1,0:T(8,128)S(1)}, f32[18,1536]{1,0:T(8,128)}, u32[]{:S(2)}) copy-start(f32[18,1536]{1,0:T(8,128)} %copy-done.22) | copy-start | bytes 331780
  596.9 8.7 %copy-start.6 = (f32[18,6144]{1,0:T(8,128)S(1)}, f32[18,6144]{1,0:T(8,128)}, u32[]{:S(2)}) copy-start(f32[18,6144]{1,0:T(8,128)} %copy-done.5) | copy-start | bytes 1327108
  596.9 11.4 %copy-start.21 = (f32[18,1536]{1,0:T(8,128)S(1)}, f32[18,1536]{1,0:T(8,128)}, u32[]{:S(2)}) copy-start(f32[18,1536]{1,0:T(8,128)} %copy-done.20) | copy-start | bytes 331780
  596.9 12.7 %copy-start.4 = (f32[18,6144]{1,0:T(8,128)S(1)}, f32[18,6144]{1,0:T(8,128)}, u32[]{:S(2)}) copy-start(f32[18,6144]{1,0:T(8,128)} %copy-done.3) | copy-start | bytes 1327108
  599.1 9.8 %copy-start.31 = (f32[48,576]{1,0:T(8,128)S(1)}, f32[48,576]{1,0:T(8,128)}, u32[]{:S(2)}) copy-start(f32[48,576]{1,0:T(8,128)} %copy-done.30) | copy-start | bytes 331780
  599.1 11.3 %copy-start.12 = (f32[192,576]{1,0:T(8,128)S(1)}, f32[192,576]{1,0:T(8,128)}, u32[]{:S(2)}) copy-start(f32[192,576]{1,0:T(8,128)} %copy-done.11) | copy-start | bytes 1327108
  599.1 12.1 %copy-start.19 = (f32[18,1536]{1,0:T(8,128)S(1)}, f32[18,1536]{1,0:T(8,128)}, u32[]{:S(2)}) copy-start(f32[18,1536]{1,0:T(8,128)} %copy-done.18) | copy-start | bytes 331780
  599.1 12.7 %copy-start.29 = (f32[48,576]{1,0:T(8,128)S(1)}, f32[48,576]{1,0:T(8,128)}, u32[]{:S(2)}) copy-start(f32[48,576]{1,0:T(8,128)} %copy-done.28) | copy-start | bytes 331780
  (13 other events, 9.6 us)
Sparse Core Ops, SparseCore 0:
  190.8 117.9 reduce-scatter.6
  314.8 113.4 reduce-scatter.4

commit v2 on v1

v2 whole, which is shorter than its diff:
```python
import jax
import jax.numpy as jnp
from jax import lax
from jax.experimental import pallas as pl
from jax.experimental.pallas import tpu as pltpu
from jax.sharding import PartitionSpec as P

ADAM_STEP = 10
BETA_ONE = 0.9
BETA_TWO = 0.95
ADAM_EPS = 1e-8
NORM_EPS = 1e-6
BIAS_ONE = 1.0 - BETA_ONE ** ADAM_STEP
BIAS_TWO = 1.0 - BETA_TWO ** ADAM_STEP
INV_SQRT2 = 0.7071067811865476
INV_SQRT2PI = 0.3989422804014327
DP_SIZE = 32
MESH_ID = pl.DeviceIdType.MESH
W1_ROWS = 48 * 18
W3_ROWS = 12 * 18
PACK_ROWS = 1088
CHUNKS = 12
CHUNK_W = 512
ROWS_DEV = 4096
TILE_R = 512
LANES = 128
MODEL_DIM = 576
GROUP_ROWS = 72
HALF_ROWS = 288
OWN_ROWS = 18
Z_SIZE = 4
PAIR = 2
ACC_SLOTS = 3
Z_PEERS = 3
PAD_ROWS = 24
WIDE_DIM = 6144
FF_DIM = 1536
STACK_ROWS = 240
TALL_ROWS = 192
SHORT_ROWS = 48


def gelu_value(pre_act):
    pre_wide = pre_act.astype(jnp.float32)
    return 0.5 * pre_wide * (1.0 + lax.erf(pre_wide * INV_SQRT2))


def device_of(core, x_pos, y_pos, z_pos):
    return ((z_pos * PAIR + y_pos) * PAIR + x_pos) * PAIR + core


def adam_new(g_val, p_val, m_val, v_val, s_val, lr_val):
    scaled = s_val * (g_val * (1.0 / DP_SIZE))
    mom_new = BETA_ONE * m_val + (1.0 - BETA_ONE) * scaled
    var_new = BETA_TWO * v_val + (1.0 - BETA_TWO) * scaled * scaled
    return p_val - lr_val * (mom_new / BIAS_ONE) / (jnp.sqrt(var_new / BIAS_TWO) + ADAM_EPS), mom_new, var_new


def update_kernel(*refs):
    sources, (lr_ref, clip_ref, all_p, all_q, norm_ref), locals_, rest = refs[:16], refs[16:21], refs[21:37], refs[37:]
    wide_p, own_p, own_q, norm_send, norm_recv, norm_ssem, norm_rsem, send_p, recv_p, send_q, recv_q, local_sem, load_sem = rest
    g1, g2, g3, g4, p1, p2, p3, p4, m1, m2, m3, m4, v1, v2, v3, v4 = locals_
    loads = [pltpu.make_async_copy(src, dst, load_sem.at[i]) for i, (src, dst) in enumerate(zip(sources, locals_))]
    for copy in loads:
        copy.start()
    me = lax.axis_index('dp')
    core = me % PAIR
    x_pos = (me // PAIR) % PAIR
    y_pos = (me // Z_SIZE) % PAIR
    z_pos = me // 8
    core_peer = device_of(1 - core, x_pos, y_pos, z_pos)
    x_peer = device_of(core, 1 - x_pos, y_pos, z_pos)
    y_peer = device_of(core, x_pos, 1 - y_pos, z_pos)
    z_others = [(z_pos + k) % Z_SIZE for k in (1, PAIR, Z_PEERS)]
    z_peers = [device_of(core, x_pos, y_pos, zo) for zo in z_others]

    barrier = pltpu.get_barrier_semaphore()
    for peer in [core_peer, x_peer, y_peer] + z_peers:
        pl.semaphore_signal(barrier, inc=1, device_id=(peer,), device_id_type=MESH_ID)
    pl.semaphore_wait(barrier, 6)

    for copy in loads:
        copy.wait()
    inv_dp = 1.0 / DP_SIZE
    total = jnp.zeros((1, LANES), jnp.float32)
    for g_ref in (g1, g3):
        for j in range(g_ref.shape[1] // LANES):
            g_val = g_ref[:, j * LANES:(j + 1) * LANES] * inv_dp
            total = total + jnp.sum(g_val * g_val, axis=0, keepdims=True)
    scal = jnp.sum(total)
    for g_ref in (g2, g4):
        g_val = g_ref[...] * inv_dp
        scal = scal + jnp.sum(g_val * g_val)
    part = jnp.full((8, LANES), scal, jnp.float32)
    for stage, peer in enumerate((core_peer, x_peer, y_peer)):
        norm_send[stage] = part
        copy = pltpu.make_async_remote_copy(src_ref=norm_send.at[stage], dst_ref=norm_recv.at[stage], send_sem=norm_ssem.at[stage], recv_sem=norm_rsem.at[stage], device_id=(peer,), device_id_type=MESH_ID)
        copy.start()
        copy.wait()
        part = part + norm_recv[stage]
    norm_send[Z_PEERS] = part
    norm_recv[Z_PEERS + z_pos] = part
    z_copies = []
    for k in range(Z_PEERS):
        z_copies.append(pltpu.make_async_remote_copy(src_ref=norm_send.at[Z_PEERS], dst_ref=norm_recv.at[Z_PEERS + z_pos], send_sem=norm_ssem.at[Z_PEERS + k], recv_sem=norm_rsem.at[Z_PEERS + z_pos], device_id=(z_peers[k],), device_id_type=MESH_ID))
        z_copies[-1].start()
    for k in range(Z_PEERS):
        pltpu.make_async_remote_copy(src_ref=norm_send.at[Z_PEERS], dst_ref=norm_recv.at[Z_PEERS + z_others[k]], send_sem=norm_ssem.at[Z_PEERS + k], recv_sem=norm_rsem.at[Z_PEERS + z_others[k]], device_id=(z_peers[k],), device_id_type=MESH_ID).wait_recv()
    for k in range(Z_PEERS):
        z_copies[k].wait_send()
    sq_all = ((norm_recv[Z_PEERS] + norm_recv[Z_SIZE]) + norm_recv[5]) + norm_recv[6]
    norm_val = jnp.sqrt(sq_all)
    norm_ref[...] = norm_val
    lr_val = lr_ref[0, 0]
    scale = jnp.minimum(1.0, clip_ref[0, 0] / (norm_val + NORM_EPS))[0:1, :]

    for base, (g_ref, p_ref, m_ref, v_ref) in ((0, (g1, p1, m1, v1)), (W1_ROWS, (g3, p3, m3, v3))):
        for j in range(g_ref.shape[1] // LANES):
            cols = slice(j * LANES, (j + 1) * LANES)
            p_new = adam_new(g_ref[:, cols], p_ref[:, cols], m_ref[:, cols], v_ref[:, cols], scale, lr_val)[0]
            wide_p[base + OWN_ROWS * j:base + OWN_ROWS * (j + 1), :] = p_new
    wide_p[W1_ROWS + W3_ROWS:, :] = jnp.zeros((PACK_ROWS - W1_ROWS - W3_ROWS, LANES), jnp.float32)
    own_p[...] = wide_p[...].astype(jnp.bfloat16)
    scale_one = scale[0:1, 0:1]
    for base, (g_ref, p_ref, m_ref, v_ref) in ((0, (g2, p2, m2, v2)), (TALL_ROWS, (g4, p4, m4, v4))):
        for r in range(g_ref.shape[0] // 16):
            rows = slice(r * 16, (r + 1) * 16)
            p_new = adam_new(g_ref[rows, :], p_ref[rows, :], m_ref[rows, :], v_ref[rows, :], scale_one, lr_val)[0]
            own_q[base + 16 * r:base + 16 * (r + 1), :] = p_new.astype(jnp.bfloat16)

    loc_p = pltpu.make_async_copy(own_p, all_p.at[me], local_sem.at[0])
    loc_q = pltpu.make_async_copy(own_q, all_q.at[me], local_sem.at[1])
    loc_p.start()
    loc_q.start()

    pending = []

    def send(buf, own, ssem, rsem, kind, slot, origin, peer, first):
        src = own if first else buf.at[origin]
        copy = pltpu.make_async_remote_copy(src_ref=src, dst_ref=buf.at[origin], send_sem=ssem.at[kind, slot], recv_sem=rsem.at[origin], device_id=(peer,), device_id_type=MESH_ID)
        copy.start()
        pending.append(copy)

    def arrive(buf, own, ssem, rsem, origin):
        pltpu.make_async_remote_copy(src_ref=own, dst_ref=buf.at[origin], send_sem=ssem.at[0, 0], recv_sem=rsem.at[origin], device_id=(core_peer,), device_id_type=MESH_ID).wait_recv()

    sets = ((all_p, own_p, send_p, recv_p, y_peer, x_peer, True), (all_q, own_q, send_q, recv_q, x_peer, y_peer, False))

    def origin_of(y_first, dz, da, db, dc=0):
        zo = (z_pos + dz) % Z_SIZE
        yo, xo = (da, db) if y_first else (db, da)
        return device_of((core + dc) % PAIR, (x_pos + xo) % PAIR, (y_pos + yo) % PAIR, zo)

    for buf, own, ssem, rsem, peer_a, peer_b, y_first in sets:
        send(buf, own, ssem, rsem, Z_PEERS, 0, me, peer_a, True)
        send(buf, own, ssem, rsem, Z_SIZE, 0, me, peer_b, True)
        for k in range(Z_PEERS):
            send(buf, own, ssem, rsem, k, 0, me, z_peers[k], True)
        send(buf, own, ssem, rsem, 5, 0, me, core_peer, True)
    steps = [(0, 1, 0)]
    for dz in (1, Z_PEERS, PAIR):
        steps += [(dz, 0, 0)]
    for dz in (1, Z_PEERS, PAIR):
        steps += [(dz, 1, 0)]
    for dz, da, _ in steps:
        for buf, own, ssem, rsem, peer_a, peer_b, y_first in sets:
            origin = origin_of(y_first, dz, da, 0)
            arrive(buf, own, ssem, rsem, origin)
            slot = dz * PAIR + da
            if da == 0:
                send(buf, own, ssem, rsem, Z_PEERS, dz, origin, peer_a, False)
            send(buf, own, ssem, rsem, Z_SIZE, slot, origin, peer_b, False)
            send(buf, own, ssem, rsem, 5, slot, origin, core_peer, False)
    for dz, da in [(0, 0), (0, 1), (1, 0), (Z_PEERS, 0), (PAIR, 0), (1, 1), (Z_PEERS, 1), (PAIR, 1)]:
        for buf, own, ssem, rsem, peer_a, peer_b, y_first in sets:
            origin = origin_of(y_first, dz, da, 1)
            arrive(buf, own, ssem, rsem, origin)
            send(buf, own, ssem, rsem, 5, 8 + dz * PAIR + da, origin, core_peer, False)
    for dz in range(Z_SIZE):
        for da in range(PAIR):
            for db in range(PAIR):
                for buf, own, ssem, rsem, peer_a, peer_b, y_first in sets:
                    arrive(buf, own, ssem, rsem, origin_of(y_first, dz, da, db, 1))
    for copy in pending:
        copy.wait_send()
    loc_p.wait()
    loc_q.wait()


def update_call(states, learn_rate, clip_max):
    f32 = jnp.float32
    bf16 = jnp.bfloat16
    dma = pltpu.SemaphoreType.DMA
    buf = pltpu.VMEM
    smem = pl.BlockSpec(memory_space=pltpu.SMEM)
    hbm = pl.BlockSpec(memory_space=pl.ANY)
    vmem = pl.BlockSpec(memory_space=pltpu.VMEM)
    kinds = 6
    return pl.pallas_call(
        update_kernel,
        out_shape=[jax.ShapeDtypeStruct((DP_SIZE, PACK_ROWS, LANES), bf16), jax.ShapeDtypeStruct((DP_SIZE, STACK_ROWS, MODEL_DIM), bf16), jax.ShapeDtypeStruct((8, LANES), f32)],
        in_specs=[hbm] * len(states) + [smem, smem],
        out_specs=[hbm, hbm, vmem],
        scratch_shapes=[buf(a.shape, f32) for a in states] + [
            buf((PACK_ROWS, LANES), f32), buf((PACK_ROWS, LANES), bf16), buf((STACK_ROWS, MODEL_DIM), bf16),
            buf((Z_SIZE, 8, LANES), f32), buf((7, 8, LANES), f32), dma((kinds,)), dma((7,)),
            dma((kinds, 16)), dma((DP_SIZE,)), dma((kinds, 16)), dma((DP_SIZE,)), dma((PAIR,)), dma((len(states),)),
        ],
        compiler_params=pltpu.CompilerParams(collective_id=0, has_side_effects=True, vmem_limit_bytes=60 * 1024 * 1024),
        name='adam_gather',
    )(*states, learn_rate.reshape(1, 1), clip_max.reshape(1, 1))


def scatter_kernel(z_hbm, dh_hbm, dht_hbm, xt_hbm, w2_hbm, out1, out2,
                   dh, dht, xt, zbuf, w2c, a_even, a_odd, d_even, d_odd, acc1, acc2,
                   ra0, ra1, ra2, ra3, rb0, rb1, rb2, rb3, s1a, s2a, s3a, s1b, s2b, s3b, own2, qbuf,
                   in_sem, zsem, wsem, sa_send, sa_recv, sb_send, sb_recv, za_send, za_recv, zb_send, zb_recv, ga_send, ga_recv, fix_send, fix_recv):
    f32 = jnp.float32
    me = lax.axis_index('dp')
    core = me % PAIR
    x_pos = (me // PAIR) % PAIR
    y_pos = (me // Z_SIZE) % PAIR
    z_pos = me // 8
    core_peer = device_of(1 - core, x_pos, y_pos, z_pos)
    x_peer = device_of(core, 1 - x_pos, y_pos, z_pos)
    y_peer = device_of(core, x_pos, 1 - y_pos, z_pos)
    diag_peer = device_of(1 - core, 1 - x_pos, y_pos, z_pos)
    z_others = [(z_pos + k) % Z_SIZE for k in (1, PAIR, Z_PEERS)]
    z_peers = [device_of(core, x_pos, y_pos, zo) for zo in z_others]

    big = [pltpu.make_async_copy(src, dst, in_sem.at[i]) for i, (src, dst) in enumerate(((dh_hbm, dh), (dht_hbm, dht), (xt_hbm, xt)))]

    def chunk_copies(chunk):
        slot = chunk % PAIR
        zt = chunk % Z_SIZE
        k = chunk // Z_SIZE
        copies = []
        for b in range(Z_SIZE):
            off = pl.multiple_of(384 * (Z_SIZE * zt + b) + LANES * k, LANES)
            copies.append(pltpu.make_async_copy(z_hbm.at[:, pl.ds(off, LANES)], zbuf.at[slot, b], zsem.at[slot, b]))
            copies.append(pltpu.make_async_copy(w2_hbm.at[:, pl.ds(off, LANES)], w2c.at[slot, :, pl.ds(b * LANES, LANES)], wsem.at[slot, b]))
        return copies

    big[0].start()
    for copy in chunk_copies(0):
        copy.start()
    big[1].start()
    big[PAIR].start()
    qbuf[...] = jnp.zeros(qbuf.shape, f32)

    barrier = pltpu.get_barrier_semaphore()
    for peer in [core_peer, x_peer, y_peer, diag_peer] + z_peers:
        pl.semaphore_signal(barrier, inc=1, device_id=(peer,), device_id_type=MESH_ID)
    pl.semaphore_wait(barrier, 7)
    for copy in big:
        copy.wait()

    def remote(src, dst, ssem, rsem, peer):
        return pltpu.make_async_remote_copy(src_ref=src, dst_ref=dst, send_sem=ssem, recv_sem=rsem, device_id=(peer,), device_id_type=MESH_ID)

    def pair0(chunk):
        slot = chunk % PAIR
        ring = chunk % ACC_SLOTS
        land = chunk % Z_SIZE
        return (remote(acc1.at[ring, 1 - core], ra0.at[land], sa_send.at[0, slot], sa_recv.at[0, land], core_peer),
                remote(acc2.at[ring, :, :, 1 - core], rb0.at[land], sb_send.at[0, slot], sb_recv.at[0, land], core_peer))

    def pair1(chunk):
        slot = chunk % PAIR
        land = chunk % Z_SIZE
        return (remote(s1a.at[slot, :, :, 1 - y_pos], ra1.at[land], sa_send.at[1, slot], sa_recv.at[1, land], y_peer),
                remote(s1b.at[slot, :, 1 - x_pos], rb1.at[land], sb_send.at[1, slot], sb_recv.at[1, land], x_peer))

    def pair2(chunk):
        slot = chunk % PAIR
        land = chunk % Z_SIZE
        return (remote(s2a.at[slot, 1 - x_pos], ra2.at[land], sa_send.at[PAIR, slot], sa_recv.at[PAIR, land], x_peer),
                remote(s2b.at[slot, 1 - y_pos], rb2.at[land], sb_send.at[PAIR, slot], sb_recv.at[PAIR, land], y_peer))

    def z_send_a(chunk):
        slot = chunk % PAIR
        land = chunk % Z_SIZE
        return [remote(s3a.at[slot, z_others[k]], ra3.at[land, z_pos], za_send.at[slot, k], za_recv.at[land, z_pos], z_peers[k]) for k in range(Z_PEERS)]

    def z_recv_a(chunk):
        slot = chunk % PAIR
        land = chunk % Z_SIZE
        return [remote(s3a.at[slot, z_others[k]], ra3.at[land, z_others[k]], za_send.at[slot, k], za_recv.at[land, z_others[k]], z_peers[k]) for k in range(Z_PEERS)]

    def z_send_b(chunk):
        zt = chunk % Z_SIZE
        return remote(s3b.at[chunk % PAIR], rb3.at[chunk // Z_SIZE, z_pos], zb_send.at[chunk % PAIR], zb_recv.at[chunk // Z_SIZE, z_pos], device_of(core, x_pos, y_pos, zt))

    def z_recv_b(chunk):
        return [remote(s3b.at[chunk % PAIR], rb3.at[chunk // Z_SIZE, z_others[k]], zb_send.at[chunk % PAIR], zb_recv.at[chunk // Z_SIZE, z_others[k]], z_peers[k]) for k in range(Z_PEERS)]

    lane_me = core * PAIR + x_pos
    group = ((1 - core, x_pos, core_peer), (core, 1 - x_pos, x_peer), (1 - core, 1 - x_pos, diag_peer))

    def g_send(chunk):
        slot = chunk % PAIR
        return [remote(qbuf.at[slot, gx * PAIR + gc], out1.at[lane_me, chunk], ga_send.at[slot, i], ga_recv.at[i, chunk % Z_SIZE], peer) for i, (gc, gx, peer) in enumerate(group)]

    def g_recv(chunk):
        slot = chunk % PAIR
        return [remote(qbuf.at[slot, gx * PAIR + gc], out1.at[gc * PAIR + gx, chunk], ga_send.at[slot, i], ga_recv.at[i, chunk % Z_SIZE], peer) for i, (gc, gx, peer) in enumerate(group)]

    def within(t, lead):
        return jnp.logical_and(t >= lead, t < lead + CHUNKS)

    def elementwise(slot, r, a_buf, d_buf):
        rows = pl.ds(pl.multiple_of(r * TILE_R, TILE_R), TILE_R)
        back = lax.dot_general(dh[rows, :], w2c[slot], (((1,), (0,)), ((), ())), preferred_element_type=f32).astype(jnp.bfloat16)
        for b in range(Z_SIZE):
            cols = slice(b * LANES, (b + 1) * LANES)
            wide = zbuf[slot, b, rows, :].astype(f32)
            cdf = 0.5 * (1.0 + lax.erf(wide * INV_SQRT2))
            a_buf[:, cols] = (wide * cdf).astype(jnp.bfloat16)
            slope = cdf + wide * INV_SQRT2PI * jnp.exp(-0.5 * wide * wide)
            d_buf[:, cols] = (back[:, cols].astype(f32) * slope).astype(jnp.bfloat16)

    def accumulate(ring, r, a_buf, d_buf, first):
        rows = pl.ds(pl.multiple_of(r * TILE_R, TILE_R), TILE_R)
        part1 = jnp.dot(xt[:, rows], d_buf[...], preferred_element_type=f32)
        part2 = jnp.dot(dht[:, rows], a_buf[...], preferred_element_type=f32)
        for b in range(Z_SIZE):
            c1, x1 = b // PAIR, b % PAIR
            val1 = part1[:, b * LANES:(b + 1) * LANES].reshape(Z_SIZE, PAIR, GROUP_ROWS, LANES)
            val2 = part2[:, b * LANES:(b + 1) * LANES].reshape(PAIR, HALF_ROWS, LANES)
            if first:
                acc1[ring, c1, x1] = val1
                acc2[ring, b // PAIR, b % PAIR] = val2
            else:
                acc1[ring, c1, x1] = acc1[ring, c1, x1] + val1
                acc2[ring, b // PAIR, b % PAIR] = acc2[ring, b // PAIR, b % PAIR] + val2

    n_tiles = ROWS_DEV // TILE_R

    def compute(chunk):
        slot = chunk % PAIR
        ring = chunk % ACC_SLOTS
        for copy in chunk_copies(chunk):
            copy.wait()

        @pl.when(chunk + 1 < CHUNKS)
        def _():
            for copy in chunk_copies(chunk + 1):
                copy.start()

        elementwise(slot, 0, a_even, d_even)
        elementwise(slot, 1, a_odd, d_odd)
        accumulate(ring, 0, a_even, d_even, True)

        def body(i, carry):
            elementwise(slot, PAIR * i, a_even, d_even)
            accumulate(ring, PAIR * i - 1, a_odd, d_odd, False)
            elementwise(slot, PAIR * i + 1, a_odd, d_odd)
            accumulate(ring, PAIR * i, a_even, d_even, False)
            return carry

        lax.fori_loop(1, n_tiles // PAIR, body, 0)
        accumulate(ring, n_tiles - 1, a_odd, d_odd, False)

    def step(t, carry):
        @pl.when(within(t, 11))
        def _():
            for copy in g_send(t - 11):
                copy.wait_send()
            for copy in g_recv(t - 11):
                copy.wait_recv()

        @pl.when(within(t, 9))
        def _():
            chunk = t - 9
            slot = chunk % PAIR
            land = chunk % Z_SIZE
            zt = chunk % Z_SIZE
            for copy in z_send_a(chunk):
                copy.wait_send()
            for copy in z_recv_a(chunk):
                copy.wait_recv()
            full = s3a[slot, z_pos]
            for zo in z_others:
                full = full + ra3[land, zo]
            for o in range(Z_SIZE):
                qbuf[slot, o, 0:OWN_ROWS, :] = full[OWN_ROWS * o:OWN_ROWS * (o + 1), :]
            out1[lane_me, chunk] = qbuf[slot, x_pos * PAIR + core]

            @pl.when(z_pos == zt)
            def _():
                for copy in z_recv_b(chunk):
                    copy.wait_recv()
                k = chunk // Z_SIZE
                total = s3b[slot]
                for zo in z_others:
                    total = total + rb3[k, zo]
                own2[k] = total

            @pl.when(z_pos != zt)
            def _():
                z_send_b(chunk).wait_send()

        @pl.when(within(t, 7))
        def _():
            chunk = t - 7
            slot = chunk % PAIR
            land = chunk % Z_SIZE
            for copy in pair2(chunk):
                copy.wait()
            for z in range(Z_SIZE):
                s3a[slot, z] = s2a[slot, x_pos, z] + ra2[land, z]
            s3b[slot] = s2b[slot, y_pos] + rb2[land]

        @pl.when(within(t, 5))
        def _():
            chunk = t - 5
            slot = chunk % PAIR
            land = chunk % Z_SIZE
            for copy in pair1(chunk):
                copy.wait()
            for x in range(PAIR):
                for z in range(Z_SIZE):
                    s2a[slot, x, z] = s1a[slot, x, z, y_pos] + ra1[land, x, z]
            for y in range(PAIR):
                s2b[slot, y] = s1b[slot, y, x_pos] + rb1[land, y]

        @pl.when(within(t, Z_PEERS))
        def _():
            chunk = t - Z_PEERS
            slot = chunk % PAIR
            land = chunk % Z_SIZE
            ring = chunk % ACC_SLOTS
            for copy in pair0(chunk):
                copy.wait()
            for x in range(PAIR):
                s1a[slot, x] = acc1[ring, core, x] + ra0[land, x]
            for y in range(PAIR):
                for x in range(PAIR):
                    s1b[slot, y, x] = acc2[ring, y, x, core] + rb0[land, y, x]

        for lead, copies in ((1, pair0), (Z_PEERS, pair1), (5, pair2), (7, z_send_a), (9, g_send)):
            @pl.when(within(t, lead))
            def _(lead=lead, copies=copies):
                for copy in copies(t - lead):
                    copy.start()

        @pl.when(jnp.logical_and(within(t, 7), z_pos != (t + 1) % Z_SIZE))
        def _():
            z_send_b(t - 7).start()

        @pl.when(t < CHUNKS)
        def _():
            compute(t)

        return carry

    lax.fori_loop(0, CHUNKS + 11, step, 0)

    fixes = [remote(own2.at[1 - core + i], out2.at[i, core], fix_send.at[i], fix_recv.at[i], core_peer) for i in range(PAIR)]
    for copy in fixes:
        copy.start()
    for i in range(PAIR):
        out2[i, core] = own2[core + i]
    for i in range(PAIR):
        remote(own2.at[1 - core + i], out2.at[i, 1 - core], fix_send.at[i], fix_recv.at[i], core_peer).wait()


def scatter_call(z_one, dh_two, dh_two_t, x_t, w_two):
    f32 = jnp.float32
    bf16 = jnp.bfloat16
    hbm = pl.BlockSpec(memory_space=pl.ANY)
    vmem = pl.BlockSpec(memory_space=pltpu.VMEM)
    dma = pltpu.SemaphoreType.DMA
    buf = pltpu.VMEM
    return pl.pallas_call(
        scatter_kernel,
        out_shape=[jax.ShapeDtypeStruct((Z_SIZE, CHUNKS, PAD_ROWS, LANES), f32), jax.ShapeDtypeStruct((PAIR, PAIR, HALF_ROWS, LANES), f32)],
        in_specs=[hbm] * 5,
        out_specs=[vmem, vmem],
        scratch_shapes=[
            buf((ROWS_DEV, MODEL_DIM), bf16), buf((MODEL_DIM, ROWS_DEV), bf16), buf((MODEL_DIM, ROWS_DEV), bf16),
            buf((PAIR, Z_SIZE, ROWS_DEV, LANES), bf16), buf((PAIR, MODEL_DIM, CHUNK_W), bf16),
            buf((TILE_R, CHUNK_W), bf16), buf((TILE_R, CHUNK_W), bf16), buf((TILE_R, CHUNK_W), bf16), buf((TILE_R, CHUNK_W), bf16),
            buf((ACC_SLOTS, PAIR, PAIR, Z_SIZE, PAIR, GROUP_ROWS, LANES), f32), buf((ACC_SLOTS, PAIR, PAIR, PAIR, HALF_ROWS, LANES), f32),
            buf((Z_SIZE, PAIR, Z_SIZE, PAIR, GROUP_ROWS, LANES), f32), buf((Z_SIZE, PAIR, Z_SIZE, GROUP_ROWS, LANES), f32), buf((Z_SIZE, Z_SIZE, GROUP_ROWS, LANES), f32), buf((Z_SIZE, Z_SIZE, GROUP_ROWS, LANES), f32),
            buf((Z_SIZE, PAIR, PAIR, HALF_ROWS, LANES), f32), buf((Z_SIZE, PAIR, HALF_ROWS, LANES), f32), buf((Z_SIZE, HALF_ROWS, LANES), f32), buf((Z_PEERS, Z_SIZE, HALF_ROWS, LANES), f32),
            buf((PAIR, PAIR, Z_SIZE, PAIR, GROUP_ROWS, LANES), f32), buf((PAIR, PAIR, Z_SIZE, GROUP_ROWS, LANES), f32), buf((PAIR, Z_SIZE, GROUP_ROWS, LANES), f32),
            buf((PAIR, PAIR, PAIR, HALF_ROWS, LANES), f32), buf((PAIR, PAIR, HALF_ROWS, LANES), f32), buf((PAIR, HALF_ROWS, LANES), f32),
            buf((Z_PEERS, HALF_ROWS, LANES), f32), buf((PAIR, Z_SIZE, PAD_ROWS, LANES), f32),
            dma((Z_PEERS,)), dma((PAIR, Z_SIZE)), dma((PAIR, Z_SIZE)),
            dma((Z_PEERS, PAIR)), dma((Z_PEERS, Z_SIZE)), dma((Z_PEERS, PAIR)), dma((Z_PEERS, Z_SIZE)),
            dma((PAIR, Z_PEERS)), dma((Z_SIZE, Z_SIZE)), dma((PAIR,)), dma((Z_PEERS, Z_SIZE)),
            dma((PAIR, Z_PEERS)), dma((Z_PEERS, Z_SIZE)), dma((PAIR,)), dma((PAIR,)),
        ],
        compiler_params=pltpu.CompilerParams(collective_id=1, has_side_effects=True, vmem_limit_bytes=60 * 1024 * 1024),
        cost_estimate=pl.CostEstimate(flops=100_000_000_000, bytes_accessed=80_000_000, transcendentals=50_000_000),
        name='grad_scatter',
    )(z_one, dh_two, dh_two_t, x_t, w_two)


def forward_kernel(xt_ref, dyt_ref, w1, w2t, w3, w4t, z_out, dh_out, dht_out, g3_out, g4t_out,
                   h_acc, a_even, a_odd, h_t, x_own, dy_own):
    f32 = jnp.float32
    bf16 = jnp.bfloat16

    @pl.when(pl.program_id(0) == 0)
    def _():
        g3_out[...] = jnp.zeros(g3_out.shape, f32)
        g4t_out[...] = jnp.zeros(g4t_out.shape, f32)

    def hidden(c, a_buf):
        cols = pl.ds(pl.multiple_of(c * CHUNK_W, CHUNK_W), CHUNK_W)
        z_val = jnp.dot(x_own[...], w1[:, cols], preferred_element_type=f32).astype(bf16)
        z_out[:, cols] = z_val
        a_buf[...] = gelu_value(z_val).astype(bf16)

    def project(c, a_buf, first):
        cols = pl.ds(pl.multiple_of(c * CHUNK_W, CHUNK_W), CHUNK_W)
        part = lax.dot_general(a_buf[...], w2t[:, cols], (((1,), (1,)), ((), ())), preferred_element_type=f32)
        if first:
            h_acc[...] = part
        else:
            h_acc[...] = h_acc[...] + part

    x_own[...] = xt_ref[...].T
    dy_own[...] = dyt_ref[...].T
    hidden(0, a_even)
    hidden(1, a_odd)
    project(0, a_even, True)

    def body(i, carry):
        hidden(PAIR * i, a_even)
        project(PAIR * i - 1, a_odd, False)
        hidden(PAIR * i + 1, a_odd)
        project(PAIR * i, a_even, False)
        return carry

    lax.fori_loop(1, CHUNKS // PAIR, body, 0)
    project(CHUNKS - 1, a_odd, False)
    h_two = h_acc[...].astype(bf16)
    h_t[...] = h_two.T
    dh_sum = None
    for j in range(w3.shape[1] // CHUNK_W):
        cols = slice(j * CHUNK_W, (j + 1) * CHUNK_W)
        z_three = jnp.dot(h_two, w3[:, cols], preferred_element_type=f32).astype(bf16)
        wide = z_three.astype(f32)
        cdf = 0.5 * (1.0 + lax.erf(wide * INV_SQRT2))
        a_three = (wide * cdf).astype(bf16)
        slope = cdf + wide * INV_SQRT2PI * jnp.exp(-0.5 * wide * wide)
        da_three = jnp.dot(dy_own[...], w4t[:, cols], preferred_element_type=f32).astype(bf16)
        dz_three = (da_three.astype(f32) * slope).astype(bf16)
        g4t_out[:, cols] = g4t_out[:, cols] + jnp.dot(dyt_ref[...], a_three, preferred_element_type=f32)
        g3_out[:, cols] = g3_out[:, cols] + jnp.dot(h_t[...], dz_three, preferred_element_type=f32)
        part = lax.dot_general(dz_three, w3[:, cols], (((1,), (1,)), ((), ())), preferred_element_type=f32)
        dh_sum = part if dh_sum is None else dh_sum + part
    dh_two = dh_sum.astype(bf16)
    dh_out[...] = dh_two
    dht_out[...] = dh_two.T


def forward_call(x_t, dy_t, w_one, w_two_t, w_three, w_four_t):
    f32 = jnp.float32
    bf16 = jnp.bfloat16
    buf = pltpu.VMEM
    rows_in = pl.BlockSpec((TILE_R, MODEL_DIM), lambda i: (i, 0))
    cols_out = pl.BlockSpec((MODEL_DIM, TILE_R), lambda i: (0, i))
    whole = lambda a: pl.BlockSpec(a.shape, lambda i: (0, 0), pipeline_mode=pl.Buffered(1))
    small = jax.ShapeDtypeStruct((MODEL_DIM, FF_DIM), f32)
    tall = jax.ShapeDtypeStruct((ROWS_DEV, MODEL_DIM), bf16)
    flat = jax.ShapeDtypeStruct((MODEL_DIM, ROWS_DEV), bf16)
    return pl.pallas_call(
        forward_kernel,
        grid=(ROWS_DEV // TILE_R,),
        out_shape=[jax.ShapeDtypeStruct((ROWS_DEV, WIDE_DIM), bf16), tall, flat, small, small],
        in_specs=[cols_out, cols_out] + [whole(a) for a in (w_one, w_two_t, w_three, w_four_t)],
        out_specs=[pl.BlockSpec((TILE_R, WIDE_DIM), lambda i: (i, 0)), rows_in, cols_out, whole(small), whole(small)],
        scratch_shapes=[buf((TILE_R, MODEL_DIM), f32), buf((TILE_R, CHUNK_W), bf16), buf((TILE_R, CHUNK_W), bf16), buf((MODEL_DIM, TILE_R), bf16), buf((TILE_R, MODEL_DIM), bf16), buf((TILE_R, MODEL_DIM), bf16)],
        compiler_params=pltpu.CompilerParams(vmem_limit_bytes=60 * 1024 * 1024),
        cost_estimate=pl.CostEstimate(flops=100_000_000_000, bytes_accessed=100_000_000, transcendentals=50_000_000),
        name='forward_chain',
    )(x_t, dy_t, w_one, w_two_t, w_three, w_four_t)


def unpack_kernel(p_ref, q_ref, norm_ref, lr_ref, clip_ref, *refs):
    states, (w1_out, w2t_out, w3_out, w4t_out), outs, (wide, lane_buf) = refs[:16], refs[16:20], refs[20:32], refs[32:]
    owners = p_ref.shape[0]

    @pl.when(pl.program_id(0) == 0)
    def _():
        lr_val = lr_ref[0, 0]
        scale = jnp.minimum(1.0, clip_ref[0, 0] / (norm_ref[...] + NORM_EPS))[0:1, 0:1]
        for i in range(Z_SIZE):
            g_ref, p_in, m_in, v_in = states[i::Z_SIZE]
            p_out, m_out, v_out = outs[i::Z_SIZE]
            p_out[...], m_out[...], v_out[...] = adam_new(g_ref[...], p_in[...], m_in[...], v_in[...], scale, lr_val)

    tall = jnp.concatenate([q_ref[o, :TALL_ROWS, :] for o in range(owners)], axis=0)
    w2t_out[...] = tall.T
    short = jnp.concatenate([q_ref[o, TALL_ROWS:, :] for o in range(owners)], axis=0)
    w4t_out[...] = short.T
    for o in range(owners):
        wide[o] = p_ref[o].astype(jnp.float32)
    for w_out, base in ((w1_out, 0), (w3_out, W1_ROWS)):
        for j in range(w_out.shape[1] // LANES):
            for o in range(owners):
                lane_buf[j % PAIR, o * OWN_ROWS:(o + 1) * OWN_ROWS, :] = wide[o, base + j * OWN_ROWS:base + (j + 1) * OWN_ROWS, :]
            w_out[:, j * LANES:(j + 1) * LANES] = lane_buf[j % PAIR].astype(jnp.bfloat16)


def unpack_call(all_p, all_q, norm, learn_rate, clip_max, states):
    f32 = jnp.float32
    bf16 = jnp.bfloat16
    owners = 8
    steps = DP_SIZE // owners
    fixed = lambda a: pl.BlockSpec(a.shape, lambda i: (0, 0))
    smem = pl.BlockSpec(memory_space=pltpu.SMEM)
    olds = [jax.ShapeDtypeStruct(a.shape, f32) for a in states[Z_SIZE:]]
    rows_of = lambda width: pl.BlockSpec((MODEL_DIM // steps, width), lambda i: (i, 0))
    cols_of = lambda width: pl.BlockSpec((MODEL_DIM, width // steps), lambda i: (0, i))
    return pl.pallas_call(
        unpack_kernel,
        grid=(steps,),
        out_shape=[jax.ShapeDtypeStruct((MODEL_DIM, w), bf16) for w in (WIDE_DIM, WIDE_DIM, FF_DIM, FF_DIM)] + olds,
        in_specs=[pl.BlockSpec((owners, PACK_ROWS, LANES), lambda i: (i, 0, 0)), pl.BlockSpec((owners, STACK_ROWS, MODEL_DIM), lambda i: (i, 0, 0)), fixed(norm), smem, smem] + [fixed(a) for a in states],
        out_specs=[rows_of(WIDE_DIM), cols_of(WIDE_DIM), rows_of(FF_DIM), cols_of(FF_DIM)] + [fixed(a) for a in olds],
        scratch_shapes=[pltpu.VMEM((owners, PACK_ROWS, LANES), f32), pltpu.VMEM((PAIR, owners * OWN_ROWS, LANES), f32)],
        compiler_params=pltpu.CompilerParams(vmem_limit_bytes=60 * 1024 * 1024),
        name='unpack_weights',
    )(all_p, all_q, norm, learn_rate.reshape(1, 1), clip_max.reshape(1, 1), *states)


def solution(mesh):
    row_spec = P('dp', None)
    rep_spec = P()

    def per_device(x_rows, dy_rows, w_one, w_two, w_three, w_four, master_one, master_two, master_three, master_four, m_one, m_two, m_three, m_four, v_one, v_two, v_three, v_four, learn_rate, clip_max):
        x_t, w_two_t = x_rows.T, w_two.T
        z_one, dh_two, dh_two_t, g_three, g_four_t = forward_call(x_t, dy_rows.T, w_one, w_two_t, w_three, w_four.T)
        small = jnp.concatenate([g.reshape(DP_SIZE, W3_ROWS, LANES) for g in (g_three, g_four_t.T)], axis=1)
        small_sum = lax.psum_scatter(small, 'dp', scatter_dimension=0, tiled=True).reshape(PAIR, W3_ROWS, LANES)
        s_three = small_sum[0].reshape(OWN_ROWS, FF_DIM)
        s_four = small_sum[1].reshape(SHORT_ROWS, MODEL_DIM)
        sum_one, sum_two = scatter_call(z_one, dh_two, dh_two_t, x_t, w_two_t)
        s_one = sum_one.reshape(Z_SIZE, Z_PEERS, Z_SIZE, PAD_ROWS, LANES)[:, :, :, :OWN_ROWS].transpose(Z_PEERS, PAIR, 0, 1, Z_SIZE).reshape(OWN_ROWS, WIDE_DIM)
        flat_two = sum_two.transpose(1, PAIR, 0, Z_PEERS).reshape(MODEL_DIM, 256)
        s_two = lax.dynamic_slice_in_dim(flat_two, 64 * (lax.axis_index('dp') % PAIR), TALL_ROWS, axis=1).T
        states = (s_one, s_two, s_three, s_four, master_one, master_two, master_three, master_four, m_one, m_two, m_three, m_four, v_one, v_two, v_three, v_four)
        all_p, all_q, norm = update_call(states, learn_rate, clip_max)
        outs = unpack_call(all_p, all_q, norm, learn_rate, clip_max, states)
        return (outs[0], outs[1].T, outs[2], outs[3].T) + tuple(outs[Z_SIZE:]) + (norm[0, 0],)

    in_specs = (row_spec, row_spec) + (rep_spec,) * Z_SIZE + (row_spec,) * 12 + (rep_spec, rep_spec)
    out_specs = (rep_spec,) * Z_SIZE + (row_spec,) * 12 + (rep_spec,)
    return jax.shard_map(per_device, mesh=mesh, in_specs=in_specs, out_specs=out_specs, check_vma=False)
```

time: 621 us -> 553 us (0.89)
  local copies, waits for them, and re-layouts: 87.6 us -> 22.2 us
  Pallas kernels: 516 us -> 509 us
    unnamed x89 -> x1, local copies, waits for them, and re-layouts: 72.3 us -> 1.37 us
    pallas_call x1, Pallas kernels: 228 us -> 212 us  [scatter_call(): pl.pallas_call(scatter_kernel, out_shape=[jax.ShapeDtypeStruct((Z_SIZE, C...]
  transfers between devices with their start and end apart: 2 -> 1, of which waited for: 0 -> 0; matrix products, arithmetic and copies ran while one was open for 2% -> 1% of each run, Pallas kernels for 37% -> 38%
where the time goes in v2:
time: 553 us
  Pallas kernels  509 us (92%)
  local copies, waits for them, and re-layouts  22.2 us (4%)
  between operations  15.4 us (3%)
    pallas_call x1, Pallas kernels, scatter_call(): pl.pallas_call(scatter_kernel, out_shape=[jax.ShapeDtypeStruct((Z_SIZE, C...  212 us
    pallas_call x1, Pallas kernels, forward_call(): pl.pallas_call(forward_kernel, grid=(ROWS_DEV // TILE_R,), out_shape=[jax...  157 us
    pallas_call x1, Pallas kernels, update_call(): pl.pallas_call(update_kernel, out_shape=[jax.ShapeDtypeStruct((DP_SIZE, P...  123 us
    pallas_call x1, Pallas kernels, unpack_call(): pl.pallas_call(unpack_kernel, grid=(steps,), out_shape=[jax.ShapeDtypeStr...  17.8 us
  transfers between devices with their start and end apart: 1, of which 0 were waited for; matrix products, arithmetic and copies ran while one was open for 1% of the time, Pallas kernels for 38%

profile of v2, /device:TPU:9, one launch (start us, length us, event | category | flops | bytes accessed | tf_op | source)
XLA Modules:
  0.0 552.5 jit_solution(14334783228274544597)
XLA Ops:
  7.2 0.0 reduce-scatter.2.cloned.1.call-start
  7.2 156.5 %forward_chain.1 = (bf16[4096,6144]{1,0:T(8,128)(2,1)}, bf16[4096,576]{1,0:T(8,128)(2,1)}, bf16[576,4096]{1,0:T(8,128)(2,1)}, f32[576,1536]{1,0:T(8,128)}, f32[576,1536]{1,0:T(8,128)}) custom-call(bf16[576,4096]{1,0:T(8,128)(2,1)} %bitcast.32, bf16[576,4096]{1,0:T(8,128)(2,1)} %bitcast.31, bf16[576,6144]{1,0:T(8,128)(2,1)} %w1.1, ...), custom_call_target="tpu_custom_call" | custom-call | flops 99999997952 | bytes 100000000 | tf_op jit(solution)/shard_map/forward_chain/pallas_call | solution.py:571
  163.8 5.3 copy.42
  169.1 3.7 reshape.66
  172.8 4.5 reshape.65
  177.3 5.4 pad_maximum_fusion
  182.7 0.0 reduce-scatter.2.cloned.1.call-update
  182.8 212.3 %grad_scatter.1 = (f32[4,12,24,128]{3,2,1,0:T(8,128)}, f32[2,2,288,128]{3,2,1,0:T(8,128)}) custom-call(bf16[4096,6144]{1,0:T(8,128)(2,1)} %get-tuple-element.43.z_hbm, bf16[4096,576]{1,0:T(8,128)(2,1)} %get-tuple-element.44.dh_hbm, bf16[576,4096]{1,0:T(8,128)(2,1)} %get-tuple-element.45.dht_hbm, bf16[576,4096]{1,0:T(8,128)(2,1)} %bitcast.33, ...), custom_call_target="tpu_custom_call" | custom-call | flops 99999997952 | bytes 80000000 | tf_op jit(solution)/shard_map/grad_scatter/pallas_call | solution.py:475
  395.1 1.4 copy.47
  396.4 1.1 reshape.63.refs_0_
  397.5 1.4 copy.43
  398.9 0.5 reshape.69
  400.7 0.8 dynamic-slice_bitcast_fusion.refs_1_
  401.6 0.0 reduce-scatter.2.cloned.1.call-done
  401.6 1.0 fusion
  402.5 0.7 reshape_squeeze.6.refs_2_
  403.2 0.7 reshape_squeeze.7.refs_3_
  403.9 122.8 %adam_gather.1 = (bf16[32,1088,128]{2,1,0:T(8,128)(2,1)}, bf16[32,240,576]{2,1,0:T(8,128)(2,1)}, f32[8,128]{1,0:T(8,128)}) custom-call(f32[18,6144]{1,0:T(8,128)} %reshape.63.refs_0_, f32[192,576]{1,0:T(8,128)} %dynamic-slice_bitcast_fusion.refs_1_, f32[18,1536]{1,0:T(8,128)} %reshape_squeeze.6.refs_2_, f32[48,576]{1,0:T(8,128)} %reshape_squeeze.7.refs_3_, ...), custom_call_target="tpu_custom_call" | custom-call | tf_op jit(solution)/shard_map/adam_gather/pallas_call | solution.py:199
  526.7 1.2 slice.17
  527.9 17.8 %unpack_weights.1 = (bf16[576,6144]{1,0:T(8,128)(2,1)}, bf16[576,6144]{1,0:T(8,128)(2,1)}, bf16[576,1536]{1,0:T(8,128)(2,1)}, bf16[576,1536]{1,0:T(8,128)(2,1)},...) custom-call(bf16[32,1088,128]{2,1,0:T(8,128)(2,1)} %get-tuple-elemen, ...), custom_call_target="tpu_custom_call" | custom-call | tf_op jit(solution)/shard_map/unpack_weights/pallas_call | solution.py:620
Async XLA Ops:
  7.2 394.4 %reduce-scatter.2.cloned.1.call-start = ((), (), s32[]{:S(2)}) async-start(), calls=%async_computation.1 | async-start | bytes 7299072 | tf_op jit(solution)/shard_map/reduce_scatter | solution.py:640
Sparse Core Ops, SparseCore 0:
  182.9 141.4 reduce-scatter.1

commit v3 on v2

--- a/solution.py
+++ b/solution.py
@@ -38,6 +38,8 @@
 STACK_ROWS = 240
 TALL_ROWS = 192
 SHORT_ROWS = 48
+SMALL_USED = W3_ROWS + 5 * SHORT_ROWS
+SMALL_ROWS = 480
 
 
 def gelu_value(pre_act):
@@ -498,8 +500,8 @@
     )(z_one, dh_two, dh_two_t, x_t, w_two)
 
 
-def forward_kernel(xt_ref, dyt_ref, w1, w2t, w3, w4t, z_out, dh_out, dht_out, g3_out, g4t_out,
-                   h_acc, a_even, a_odd, h_t, x_own, dy_own):
+def forward_kernel(xt_ref, dyt_ref, w1, w2t, w3, w4t, z_out, dh_out, dht_out, small_out,
+                   g3_out, g4t_out, h_acc, a_even, a_odd, h_t, x_own, dy_own):
     f32 = jnp.float32
     bf16 = jnp.bfloat16
 
@@ -557,6 +559,24 @@
     dh_out[...] = dh_two
     dht_out[...] = dh_two.T
 
+    @pl.when(pl.program_id(0) == ROWS_DEV // TILE_R - 1)
+    def _():
+        for d in range(DP_SIZE):
+            for j in range(CHUNKS):
+                small_out[d, j * OWN_ROWS:(j + 1) * OWN_ROWS, :] = g3_out[d * OWN_ROWS:(d + 1) * OWN_ROWS, j * LANES:(j + 1) * LANES]
+        small_out[:, SMALL_USED:, :] = jnp.zeros((DP_SIZE, SMALL_ROWS - SMALL_USED, LANES), f32)
+        whole_lanes = MODEL_DIM // LANES
+        rest = MODEL_DIM - whole_lanes * LANES
+        group = 8
+        for e in range(DP_SIZE // group):
+            turned = g4t_out[:, e * group * SHORT_ROWS:(e + 1) * group * SHORT_ROWS].T
+            for i in range(group):
+                rows = turned[i * SHORT_ROWS:(i + 1) * SHORT_ROWS, :]
+                for j in range(whole_lanes):
+                    small_out[e * group + i, W3_ROWS + j * SHORT_ROWS:W3_ROWS + (j + 1) * SHORT_ROWS, :] = rows[:, j * LANES:(j + 1) * LANES]
+                last = W3_ROWS + whole_lanes * SHORT_ROWS
+                small_out[e * group + i, last:SMALL_USED, :] = jnp.concatenate([rows[:, whole_lanes * LANES:], jnp.zeros((SHORT_ROWS, LANES - rest), f32)], axis=1)
+
 
 def forward_call(x_t, dy_t, w_one, w_two_t, w_three, w_four_t):
     f32 = jnp.float32
@@ -565,16 +585,16 @@
     rows_in = pl.BlockSpec((TILE_R, MODEL_DIM), lambda i: (i, 0))
     cols_out = pl.BlockSpec((MODEL_DIM, TILE_R), lambda i: (0, i))
     whole = lambda a: pl.BlockSpec(a.shape, lambda i: (0, 0), pipeline_mode=pl.Buffered(1))
-    small = jax.ShapeDtypeStruct((MODEL_DIM, FF_DIM), f32)
+    small = jax.ShapeDtypeStruct((DP_SIZE, SMALL_ROWS, LANES), f32)
     tall = jax.ShapeDtypeStruct((ROWS_DEV, MODEL_DIM), bf16)
     flat = jax.ShapeDtypeStruct((MODEL_DIM, ROWS_DEV), bf16)
     return pl.pallas_call(
         forward_kernel,
         grid=(ROWS_DEV // TILE_R,),
-        out_shape=[jax.ShapeDtypeStruct((ROWS_DEV, WIDE_DIM), bf16), tall, flat, small, small],
+        out_shape=[jax.ShapeDtypeStruct((ROWS_DEV, WIDE_DIM), bf16), tall, flat, small],
         in_specs=[cols_out, cols_out] + [whole(a) for a in (w_one, w_two_t, w_three, w_four_t)],
-        out_specs=[pl.BlockSpec((TILE_R, WIDE_DIM), lambda i: (i, 0)), rows_in, cols_out, whole(small), whole(small)],
-        scratch_shapes=[buf((TILE_R, MODEL_DIM), f32), buf((TILE_R, CHUNK_W), bf16), buf((TILE_R, CHUNK_W), bf16), buf((MODEL_DIM, TILE_R), bf16), buf((TILE_R, MODEL_DIM), bf16), buf((TILE_R, MODEL_DIM), bf16)],
+        out_specs=[pl.BlockSpec((TILE_R, WIDE_DIM), lambda i: (i, 0)), rows_in, cols_out, pl.BlockSpec(small.shape, lambda i: (0, 0, 0), pipeline_mode=pl.Buffered(1))],
+        scratch_shapes=[buf((MODEL_DIM, FF_DIM), f32), buf((MODEL_DIM, FF_DIM), f32), buf((TILE_R, MODEL_DIM), f32), buf((TILE_R, CHUNK_W), bf16), buf((TILE_R, CHUNK_W), bf16), buf((MODEL_DIM, TILE_R), bf16), buf((TILE_R, MODEL_DIM), bf16), buf((TILE_R, MODEL_DIM), bf16)],
         compiler_params=pltpu.CompilerParams(vmem_limit_bytes=60 * 1024 * 1024),
         cost_estimate=pl.CostEstimate(flops=100_000_000_000, bytes_accessed=100_000_000, transcendentals=50_000_000),
         name='forward_chain',
@@ -635,11 +655,10 @@
 
     def per_device(x_rows, dy_rows, w_one, w_two, w_three, w_four, master_one, master_two, master_three, master_four, m_one, m_two, m_three, m_four, v_one, v_two, v_three, v_four, learn_rate, clip_max):
         x_t, w_two_t = x_rows.T, w_two.T
-        z_one, dh_two, dh_two_t, g_three, g_four_t = forward_call(x_t, dy_rows.T, w_one, w_two_t, w_three, w_four.T)
-        small = jnp.concatenate([g.reshape(DP_SIZE, W3_ROWS, LANES) for g in (g_three, g_four_t.T)], axis=1)
-        small_sum = lax.psum_scatter(small, 'dp', scatter_dimension=0, tiled=True).reshape(PAIR, W3_ROWS, LANES)
-        s_three = small_sum[0].reshape(OWN_ROWS, FF_DIM)
-        s_four = small_sum[1].reshape(SHORT_ROWS, MODEL_DIM)
+        z_one, dh_two, dh_two_t, small = forward_call(x_t, dy_rows.T, w_one, w_two_t, w_three, w_four.T)
+        small_sum = lax.psum_scatter(small.reshape(-1, LANES), 'dp', scatter_dimension=0, tiled=True)
+        s_three = small_sum[:W3_ROWS].reshape(CHUNKS, OWN_ROWS, LANES).transpose(1, 0, 2).reshape(OWN_ROWS, FF_DIM)
+        s_four = small_sum[W3_ROWS:SMALL_USED].reshape(5, SHORT_ROWS, LANES).transpose(1, 0, 2).reshape(SHORT_ROWS, 5 * LANES)[:, :MODEL_DIM]
         sum_one, sum_two = scatter_call(z_one, dh_two, dh_two_t, x_t, w_two_t)
         s_one = sum_one.reshape(Z_SIZE, Z_PEERS, Z_SIZE, PAD_ROWS, LANES)[:, :, :, :OWN_ROWS].transpose(Z_PEERS, PAIR, 0, 1, Z_SIZE).reshape(OWN_ROWS, WIDE_DIM)
         flat_two = sum_two.transpose(1, PAIR, 0, Z_PEERS).reshape(MODEL_DIM, 256)

time: 553 us -> 538 us (0.973)
  local copies, waits for them, and re-layouts: 22.2 us -> 9.59 us
    reshape x2, local copies, waits for them, and re-layouts: 8.23 us -> 0.66 us  [the longest x1 0.65 us: per_device(): small_sum[W3_ROWS:SMALL_USED].reshape(5, SHORT_ROWS, LANES)]
  transfers between devices with their start and end apart: 1 -> 1, of which waited for: 0 -> 0; matrix products, arithmetic and copies ran while one was open for 1% -> 1% of each run, Pallas kernels for 38% -> 39%
where the time goes in v3:
time: 538 us
  Pallas kernels  513 us (95%)
  between operations  15.4 us (3%)
  local copies, waits for them, and re-layouts  9.59 us (2%)
    pallas_call x1, Pallas kernels, scatter_call(): pl.pallas_call(scatter_kernel, out_shape=[jax.ShapeDtypeStruct((Z_SIZE, C...  212 us
    pallas_call x1, Pallas kernels, forward_call(): pl.pallas_call(forward_kernel, grid=(ROWS_DEV // TILE_R,), out_shape=[jax...  160 us
    pallas_call x1, Pallas kernels, update_call(): pl.pallas_call(update_kernel, out_shape=[jax.ShapeDtypeStruct((DP_SIZE, P...  123 us
    pallas_call x1, Pallas kernels, unpack_call(): pl.pallas_call(unpack_kernel, grid=(steps,), out_shape=[jax.ShapeDtypeStr...  17.8 us
  transfers between devices with their start and end apart: 1, of which 0 were waited for; matrix products, arithmetic and copies ran while one was open for 1% of the time, Pallas kernels for 39%

profile of v3, /device:TPU:9, one launch (start us, length us, event | category | flops | bytes accessed | tf_op | source)
XLA Modules:
  0.0 537.9 jit_solution(13722589771000024278)
XLA Ops:
  7.2 0.0 reduce-scatter.2.cloned.1.call-start
  7.2 160.1 %forward_chain.1 = (bf16[4096,6144]{1,0:T(8,128)(2,1)}, bf16[4096,576]{1,0:T(8,128)(2,1)}, bf16[576,4096]{1,0:T(8,128)(2,1)}, f32[32,480,128]{2,1,0:T(8,128)}) custom-call(bf16[576,4096]{1,0:T(8,128)(2,1)} %bitcast.51, bf16[576,4096]{1,0:T(8,128)(2,1)} %bitcast.50, bf16[576,6144]{1,0:T(8,128)(2,1)} %w1.1, bf16[576,6144]{1,0:T(8,128)(2,1)} %bitcast.47, ...), custom_call_target="tpu_custom_call" | custom-call | flops 99999997952 | bytes 100000000 | tf_op jit(solution)/shard_map/forward_chain/pallas_call | solution.py:591
  167.4 0.0 reduce-scatter.2.cloned.1.call-update
  167.4 212.2 %grad_scatter.1 = (f32[4,12,24,128]{3,2,1,0:T(8,128)}, f32[2,2,288,128]{3,2,1,0:T(8,128)}) custom-call(bf16[4096,6144]{1,0:T(8,128)(2,1)} %get-tuple-element.42.z_hbm, bf16[4096,576]{1,0:T(8,128)(2,1)} %get-tuple-element.43.dh_hbm, bf16[576,4096]{1,0:T(8,128)(2,1)} %get-tuple-element.44.dht_hbm, bf16[576,4096]{1,0:T(8,128)(2,1)} %bitcast.52, ...), custom_call_target="tpu_custom_call" | custom-call | flops 99999997952 | bytes 80000000 | tf_op jit(solution)/shard_map/grad_scatter/pallas_call | solution.py:477
  379.6 1.4 copy.51
  381.0 1.1 reshape.67.refs_0_
  382.0 1.4 copy.44
  383.5 0.5 reshape.76
  385.3 0.8 dynamic-slice_bitcast_fusion.refs_1_
  386.1 0.0 reduce-scatter.2.cloned.1.call-done
  386.1 0.9 slice.21
  387.1 0.7 copy.48
  387.8 0.9 slice.22
  388.7 0.6 copy.52
  389.4 122.7 %adam_gather.1 = (bf16[32,1088,128]{2,1,0:T(8,128)(2,1)}, bf16[32,240,576]{2,1,0:T(8,128)(2,1)}, f32[8,128]{1,0:T(8,128)}) custom-call(f32[18,6144]{1,0:T(8,128)} %reshape.67.refs_0_, f32[192,576]{1,0:T(8,128)} %dynamic-slice_bitcast_fusion.refs_1_, f32[18,1536]{1,0:T(8,128)} %bitcast.38, f32[48,576]{1,0:T(8,128)} %bitcast.40, f32[18,6144]{1,0:T(8,128)} %refs_4_.3, ...), custom_call_target="tpu_custom_call" | custom-call | tf_op jit(solution)/shard_map/adam_gather/pallas_call | solution.py:201
  512.1 1.2 slice.19
  513.3 17.8 %unpack_weights.1 = (bf16[576,6144]{1,0:T(8,128)(2,1)}, bf16[576,6144]{1,0:T(8,128)(2,1)}, bf16[576,1536]{1,0:T(8,128)(2,1)}, bf16[576,1536]{1,0:T(8,128)(2,1)},...) custom-call(bf16[32,1088,128]{2,1,0:T(8,128)(2,1)} %get-tuple-elemen, ...), custom_call_target="tpu_custom_call" | custom-call | tf_op jit(solution)/shard_map/unpack_weights/pallas_call | solution.py:640
  (3 shorter events, 0.1 us)
Async XLA Ops:
  7.2 378.9 %reduce-scatter.2.cloned.1.call-start = ((), (), s32[]{:S(2)}) async-start(), calls=%async_computation.1 | async-start | bytes 8110080 | tf_op jit(solution)/shard_map/reduce_scatter | solution.py:659
Sparse Core Ops, SparseCore 0:
  167.5 149.2 reduce-scatter.1
